TPU v7x, 512 devices: a whole 4x4x16 slice. The times are simulated.
512 devices in a mesh: scen: 32 (over z, core), grp: 16 (over x, y).
Axes of the slice: x: 4, y: 4, z: 16, core: 2. Of those that a mesh axis runs over, the one named last changes fastest.
Arguments:
- borders: bfloat16 [192, 512, 2048], P('scen', None, 'grp'), may hold values from -0.25 to 0.25
- row_scale: float32 [192, 512], P('scen'), may hold values from 0.1 to 10
- assign: int32 [192], P('scen'), may hold values from 0 to 191, each once
- prob: float32 [192], replicated, may hold values from 0.5 to 2
- pattern: int32 [192, 16], replicated, may hold values 0 or 1
- first_diag: float32 [2048], replicated, may hold values from 0.1 to 2
- rhs: float32 [2048], replicated, may hold values from -6 to 6
Outputs:
- schur: float32 [2048, 2048], P('scen', 'grp')
- solution: float32 [2048], replicated
Inputs may be any that keep to these rules, and one draw needn't show every extreme that they name: `assign`: each scenario number appears in exactly one slot.
All inputs are finite; a program needn't handle non-finite values.
Results may differ from a plain program's by a relative error of at most 0.00053.
Values may be sent and summed in bfloat16 or wider, within the bound.
A program may use at most 64 MiB of HBM per device.

v0:
```python
import jax
import jax.numpy as jnp
from jax import lax
from jax.sharding import PartitionSpec as P

ITERS = 5


def split_up(shard, dim, size):
    shape = shard.shape
    blocks = shard.reshape(*shape[:dim], size, shape[dim] // size, *shape[dim + 1 :])
    return jnp.moveaxis(blocks, dim, 0)


def summed_on_arrival(shard, axis, dim):
    blocks = split_up(shard, dim, lax.axis_size(axis))
    arrived = lax.all_to_all(blocks, axis, split_axis=0, concat_axis=0, tiled=True)
    return arrived.sum(axis=0)


def from_everyone(shard, axis):
    copies = jnp.broadcast_to(shard, (lax.axis_size(axis), *shard.shape))
    return lax.all_to_all(copies, axis, split_axis=0, concat_axis=0, tiled=True)


def of_everyone(shard, axis):
    return from_everyone(shard, axis).sum(axis=0)


def joined_along(blocks, dim):
    shape = list(blocks.shape[1:])
    shape[dim] *= blocks.shape[0]
    return jnp.moveaxis(blocks, 0, dim).reshape(shape)


def gathered_copies(shard, axis, dim):
    blocks = from_everyone(shard, axis)
    return joined_along(blocks, dim)


def on_device(borders, row_scale, assign, prob, pattern, first_diag, rhs):
    cols = borders.shape[2]
    full = cols * lax.axis_size("grp")
    tiles = pattern.shape[1]
    tile_cols = full // tiles
    scen_total = prob.shape[0]
    onehot = (assign[:, None] == jnp.arange(scen_total, dtype=jnp.int32)[None, :]).astype(
        jnp.float32
    )
    weight = jnp.dot(onehot, prob, precision=lax.Precision.HIGHEST)
    pat_rows = jnp.dot(onehot, pattern.astype(jnp.float32), precision=lax.Precision.HIGHEST)
    start_col = lax.axis_index("grp") * cols
    col_ids = start_col + jnp.arange(cols, dtype=jnp.int32)
    col_tile = col_ids // tile_cols
    tile_table = (jnp.arange(tiles, dtype=jnp.int32)[:, None] == col_tile[None, :]).astype(
        jnp.float32
    )
    keep = jnp.dot(pat_rows, tile_table, precision=lax.Precision.HIGHEST)
    masked = borders * keep[:, None, :].astype(jnp.bfloat16)
    factor = row_scale * (weight / scen_total)[:, None]
    scaled = (masked.astype(jnp.float32) * factor[:, :, None]).astype(jnp.bfloat16)
    stripe = jnp.einsum(
        "krm,krj->mj",
        lax.all_gather(masked, "grp", axis=2, tiled=True),
        scaled,
        preferred_element_type=jnp.float32,
    )
    rows_blk = full // lax.axis_size("scen")
    row_first = lax.axis_index("scen") * rows_blk
    row_ids = row_first + jnp.arange(rows_blk, dtype=jnp.int32)
    diag_rows = lax.dynamic_slice_in_dim(first_diag, row_first, rows_blk)
    on_block_diag = row_ids[:, None] == col_ids[None, :]
    block = summed_on_arrival(stripe, "scen", 0)
    schur = block + jnp.where(on_block_diag, diag_rows[:, None], 0.0)
    solution = jnp.zeros_like(rhs)
    residual = rhs
    direction = rhs
    norm_now = jnp.dot(residual, residual, precision=lax.Precision.HIGHEST)
    for step in range(ITERS):
        own = lax.dynamic_slice_in_dim(direction, start_col, cols)
        partial_rows = jnp.dot(schur, own, precision=lax.Precision.HIGHEST)
        summed = of_everyone(partial_rows, "grp")
        image = gathered_copies(summed, "scen", 0)
        alpha = norm_now / jnp.dot(direction, image, precision=lax.Precision.HIGHEST)
        solution = solution + alpha * direction
        residual = residual - alpha * image
        norm_next = jnp.dot(residual, residual, precision=lax.Precision.HIGHEST)
        direction = residual + norm_next / norm_now * direction
        norm_now = norm_next
    return (schur, solution)


def solution(mesh):
    placed = (P("scen", None, "grp"), P("scen", None), P("scen"), P(), P(), P(), P())
    return jax.shard_map(
        on_device, mesh=mesh, in_specs=placed, out_specs=(P("scen", "grp"), P()), check_vma=False
    )
```

profile of v0, /device:TPU:1, one launch (start us, length us, event | category | flops | bytes accessed | tf_op | source)
XLA Modules:
  0.0 361.8 jit_solution(9787978796221144077)
XLA Ops:
  7.3 1.4 copy.13
  8.7 0.9 fusion.3
  9.7 1.1 broadcast_multiply_fusion
  10.8 0.8 fusion
  11.7 0.8 broadcast_multiply_fusion.1
  12.5 108.8 %all-gather.2.cloned.1.call-done = bf16[6,512,2048]{1,2,0:T(8,128)(2,1)} async-done(((bf16[6,512,128]{1,2,0:T(8,128)(2,1)}), bf16[6,512,2048]{1,2,0:T(8,128)(2,1)}) %all-gather.2.cloned.1.call-update) | async-done | bytes 12582928 | tf_op jit(solution)/shard_map/all_gather | solution.py:64
  121.3 9.2 %fusion.1 = f32[2048,128,1]{1,0,2:T(8,128)} fusion(bf16[6,512,2048]{1,2,0:T(8,128)(2,1)} %all-gather.2.cloned.1.call-done, bf16[6,512,128]{1,2,0:T(8,128)(2,1)} %broadcast_multiply_fusion, f32[6,512]{1,0:T(8,128)S(1)} %broadcast_multiply_fusion.1), kind=kOutput, calls=%fused_computation.9 | convolution fusion | flops 1611792384 | bytes 14430208 | tf_op jit(solution)/shard_map/krm,krj->mj/dot_general | solution.py:62
  130.5 13.2 %all-to-all-start = ((f32[32,64,128]{2,1,0:T(8,128)}), f32[32,64,128]{2,1,0:T(8,128)S(1)}, u32[]{:S(2)}, u32[]{:S(2)}) async-start(f32[32,64,128]{2,1,0:T(8,128)} %bitcast.3), calls=%async_computation | async-start | bytes 2097152 | tf_op jit(solution)/shard_map/all_to_all | solution.py:17
  143.7 0.8 dynamic_slice.18
  144.5 54.9 %all-to-all-done = f32[32,64,128]{2,1,0:T(8,128)S(1)} async-done(((f32[32,64,128]{2,1,0:T(8,128)}), f32[32,64,128]{2,1,0:T(8,128)S(1)}, u32[]{:S(2)}, u32[]{:S(2)}) %all-to-all-start) | async-done | bytes 1048608 | tf_op jit(solution)/shard_map/all_to_all | solution.py:17
  199.8 11.2 %all_to_all.65 = f32[16,1,64]{2,1,0:T(1,128)S(1)} all-to-all(f32[16,1,64]{2,1,0:T(1,128)S(1)} %broadcast_in_dim.54), channel_id=1, replica_groups=mesh['scen'=32,'grp'=16] {'grp'}, dimensions={0} | all-to-all | bytes 8192 | tf_op jit(solution)/shard_map/all_to_all | solution.py:23
  211.1 16.5 %all_to_all.66 = f32[32,1,64]{2,1,0:T(1,128)S(1)} all-to-all(f32[32,1,64]{2,1,0:T(1,128)S(1)} %broadcast_in_dim.55), channel_id=1, replica_groups=mesh['scen'=32,'grp'=16] {'scen'}, dimensions={0} | all-to-all | bytes 16384 | tf_op jit(solution)/shard_map/all_to_all | solution.py:23
  228.1 0.7 reduce.40
  228.8 0.7 multiply_reduce_fusion.8
  230.8 0.7 multiply_reduce_fusion.7
  233.0 9.2 %all_to_all.67 = f32[16,1,64]{2,1,0:T(1,128)S(1)} all-to-all(f32[16,1,64]{2,1,0:T(1,128)S(1)} %broadcast_in_dim.56), channel_id=1, replica_groups=mesh['scen'=32,'grp'=16] {'grp'}, dimensions={0} | all-to-all | bytes 8192 | tf_op jit(solution)/shard_map/all_to_all | solution.py:23
  242.2 16.8 %all_to_all.68 = f32[32,1,64]{2,1,0:T(1,128)S(1)} all-to-all(f32[32,1,64]{2,1,0:T(1,128)S(1)} %broadcast_in_dim.57), channel_id=1, replica_groups=mesh['scen'=32,'grp'=16] {'scen'}, dimensions={0} | all-to-all | bytes 16384 | tf_op jit(solution)/shard_map/all_to_all | solution.py:23
  259.1 0.7 reduce.41
  259.8 0.6 multiply_reduce_fusion.6
  263.9 9.2 %all_to_all.69 = f32[16,1,64]{2,1,0:T(1,128)S(1)} all-to-all(f32[16,1,64]{2,1,0:T(1,128)S(1)} %broadcast_in_dim.58), channel_id=1, replica_groups=mesh['scen'=32,'grp'=16] {'grp'}, dimensions={0} | all-to-all | bytes 8192 | tf_op jit(solution)/shard_map/all_to_all | solution.py:23
  273.1 16.8 %all_to_all.70 = f32[32,1,64]{2,1,0:T(1,128)S(1)} all-to-all(f32[32,1,64]{2,1,0:T(1,128)S(1)} %broadcast_in_dim.59), channel_id=1, replica_groups=mesh['scen'=32,'grp'=16] {'scen'}, dimensions={0} | all-to-all | bytes 16384 | tf_op jit(solution)/shard_map/all_to_all | solution.py:23
  289.9 0.7 reduce.42
  290.7 0.7 multiply_reduce_fusion.4
  292.6 0.7 multiply_reduce_fusion.3
  294.9 9.2 %all_to_all.71 = f32[16,1,64]{2,1,0:T(1,128)S(1)} all-to-all(f32[16,1,64]{2,1,0:T(1,128)S(1)} %broadcast_in_dim.60), channel_id=1, replica_groups=mesh['scen'=32,'grp'=16] {'grp'}, dimensions={0} | all-to-all | bytes 8192 | tf_op jit(solution)/shard_map/all_to_all | solution.py:23
  304.1 16.8 %all_to_all.72 = f32[32,1,64]{2,1,0:T(1,128)S(1)} all-to-all(f32[32,1,64]{2,1,0:T(1,128)S(1)} %broadcast_in_dim.61), channel_id=1, replica_groups=mesh['scen'=32,'grp'=16] {'scen'}, dimensions={0} | all-to-all | bytes 16384 | tf_op jit(solution)/shard_map/all_to_all | solution.py:23
  320.9 0.7 reduce.43
  325.7 9.2 %all_to_all.73 = f32[16,1,64]{2,1,0:T(1,128)S(1)} all-to-all(f32[16,1,64]{2,1,0:T(1,128)S(1)} %broadcast_in_dim.62), channel_id=1, replica_groups=mesh['scen'=32,'grp'=16] {'grp'}, dimensions={0} | all-to-all | bytes 8192 | tf_op jit(solution)/shard_map/all_to_all | solution.py:23
  334.9 16.8 %all_to_all.74 = f32[32,1,64]{2,1,0:T(1,128)S(1)} all-to-all(f32[32,1,64]{2,1,0:T(1,128)S(1)} %broadcast_in_dim.63), channel_id=1, replica_groups=mesh['scen'=32,'grp'=16] {'scen'}, dimensions={0} | all-to-all | bytes 16384 | tf_op jit(solution)/shard_map/all_to_all | solution.py:23
  351.7 0.7 reduce.44
  352.5 0.6 multiply_reduce_fusion
  354.4 0.6 multiply_add_fusion
  (47 shorter events, 4.4 us)
Async XLA Ops:
  7.2 3.7 %copy-start = (f32[192]{0:T(256)S(1)}, f32[192]{0:T(256)}, u32[]{:S(2)}) copy-start(f32[192]{0:T(256)} %param.10) | copy-start | bytes 2308
  7.2 192.4 %copy-start.2 = (f32[2048]{0:T(1024)S(1)}, f32[2048]{0:T(1024)}, u32[]{:S(2)}) copy-start(f32[2048]{0:T(1024)} %param.13) | copy-start | bytes 24580
  7.2 114.1 %all-gather.2.cloned.1.call-start = ((), (), s32[]{:S(2)}) async-start(), calls=%async_computation.11 | async-start | bytes 13369344 | tf_op jit(solution)/shard_map/all_gather | solution.py:64
  130.5 68.9 %all-to-all-start = ((f32[32,64,128]{2,1,0:T(8,128)}), f32[32,64,128]{2,1,0:T(8,128)S(1)}, u32[]{:S(2)}, u32[]{:S(2)}) async-start(f32[32,64,128]{2,1,0:T(8,128)} %bitcast.3), calls=%async_computation | async-start | bytes 2097152 | tf_op jit(solution)/shard_map/all_to_all | solution.py:17
  199.6 155.4 %copy-start.1 = (f32[64,128]{1,0:T(8,128)}, f32[64,128]{1,0:T(8,128)S(1)}, u32[]{:S(2)}) copy-start(f32[64,128]{1,0:T(8,128)S(1)} %select_add_fusion) | copy-start | bytes 98308
Sparse Core Ops, SparseCore 0:
  11.1 110.1 all-gather.1
where the time goes:
time: 363 us; the launch traced here: 362 us
  waiting for transfers between devices  164 us (45%)
  blocking collectives  132 us (36%)
  between operations  25.8 us (7%)
  starting transfers between devices  13.2 us (4%)
  matrix products  12.1 us (3%)
  other arithmetic  11.9 us (3%)
    all_to_all x10, blocking collectives, from_everyone(): return lax.all_to_all(copies, axis, split_axis=0, concat_axis=0, tiled=True)  132 us
    all_gather x1, waiting for transfers between devices, on_device(): lax.all_gather(masked, 'grp', axis=2, tiled=True)  109 us
    all_to_all x1, waiting for transfers between devices, summed_on_arrival(): lax.all_to_all(blocks, axis, split_axis=0, concat_axis=0, tiled=True)  54.9 us
    all_to_all x1, starting transfers between devices, summed_on_arrival(): lax.all_to_all(blocks, axis, split_axis=0, concat_axis=0, tiled=True)  13.2 us
    dot_general x1, matrix products, on_device(): jnp.einsum('krm,krj->mj', lax.all_gather(masked, 'grp', axis=2, tiled=Tru...  9.2 us
  transfers between devices with their start and end apart: 2, of which 2 were waited for; matrix products, arithmetic and copies ran while one was open for 1% of the time, Pallas kernels for 0%

commit v1 on v0

v1 whole, which is shorter than its diff:
```python
import jax
import jax.numpy as jnp
from jax import lax
from jax.experimental import pallas as pl
from jax.experimental.pallas import tpu as pltpu
from jax.sharding import PartitionSpec as P


ITERS = 5
SIDE = 4
DEPTH = 16
KS = 6
R = 512
T = 128
HALF = R // 2
NCHUNK = 16
CROWS = 64
MESH = pl.DeviceIdType.MESH
F32 = jnp.float32
BF16 = jnp.bfloat16


def kernel(
    assign_ref,
    prob_ref,
    pattern_ref,
    b_ref,
    rs_ref,
    fd_ref,
    rhs_ref,
    schur_ref,
    sol_ref,
    rowbuf,
    colbuf,
    fac,
    acc,
    core_in,
    part,
    near_in,
    near_sum,
    far_in,
    mine,
    own_block,
    block,
    dvec,
    msg,
    inbox,
    tally,
    g_send,
    g_recv,
    c_send,
    c_recv,
    na_send,
    na_recv,
    fa_send,
    fa_recv,
    fb_send,
    fb_recv,
    nb_send,
    nb_recv,
    o_send,
    o_recv,
    m_send,
    m_recv,
):
    scen = lax.axis_index("scen")
    grp = lax.axis_index("grp")
    z = scen // 2
    c = lax.rem(scen, 2)
    x = grp // SIDE
    y = lax.rem(grp, SIDE)

    def at(xx, yy, zz, cc):
        return (2 * zz + cc, SIDE * xx + yy)

    def up(v, by, n):
        return lax.rem(v + by, n)

    def remote(src, dst, send, recv, dev):
        return pltpu.make_async_remote_copy(
            src_ref=src, dst_ref=dst, send_sem=send, recv_sem=recv, device_id=dev, device_id_type=MESH
        )

    jl, jh, jx = z // 8, lax.rem(z // 4, 2), lax.rem(z, 4)
    to_z = 4 * x + 2 * c + jl
    out_to = at(jx, y, to_z, jh)
    out_from = at(z // 4, y, (lax.rem(z, 2) * 2 + c) * 4 + x, lax.rem(z, 4) // 2)
    stays = (out_to[0] == scen) & (out_to[1] == grp)

    def plane_peer(i):
        p = lax.rem(2 * grp + c + i, 32)
        return (2 * z + lax.rem(p, 2), p // 2)

    barrier = pltpu.get_barrier_semaphore()

    def greet(i, carry):
        pl.semaphore_signal(barrier, inc=1, device_id=plane_peer(i), device_id_type=MESH)
        return carry

    lax.fori_loop(1, 32, greet, 0)
    for by in (1, 2, 4, 8, 12, 14, 15):
        pl.semaphore_signal(barrier, inc=1, device_id=at(x, y, up(z, by, DEPTH), c), device_id_type=MESH)

    @pl.when(jnp.logical_not(stays))
    def _():
        pl.semaphore_signal(barrier, inc=1, device_id=out_to, device_id_type=MESH)
        pl.semaphore_signal(barrier, inc=1, device_id=out_from, device_id_type=MESH)

    pl.semaphore_wait(barrier, jnp.where(stays, 38, 40))

    xp, xm, yp, ym = up(x, 1, SIDE), up(x, 3, SIDE), up(y, 1, SIDE), up(y, 3, SIDE)

    def own(k):
        return (
            remote(b_ref.at[k], colbuf.at[x, k], g_send.at[0, k], g_recv.at[0, k], at(xp, y, z, c)),
            remote(b_ref.at[k], colbuf.at[x, k], g_send.at[1, k], g_recv.at[1, k], at(xm, y, z, c)),
            remote(b_ref.at[k], rowbuf.at[y, k], g_send.at[4, k], g_recv.at[4, k], at(x, yp, z, c)),
            remote(b_ref.at[k], rowbuf.at[y, k], g_send.at[5, k], g_recv.at[5, k], at(x, ym, z, c)),
        )

    lo, hi = pl.ds(0, HALF), pl.ds(HALF, HALF)

    def onward(k):
        return (
            remote(colbuf.at[xm, k, lo], colbuf.at[xm, k, lo], g_send.at[2, k], g_recv.at[2, k], at(xp, y, z, c)),
            remote(colbuf.at[xp, k, hi], colbuf.at[xp, k, hi], g_send.at[3, k], g_recv.at[3, k], at(xm, y, z, c)),
            remote(rowbuf.at[ym, k, lo], rowbuf.at[ym, k, lo], g_send.at[6, k], g_recv.at[6, k], at(x, yp, z, c)),
            remote(rowbuf.at[yp, k, hi], rowbuf.at[yp, k, hi], g_send.at[7, k], g_recv.at[7, k], at(x, ym, z, c)),
        )

    def arrive_own(k):
        remote(b_ref.at[k], colbuf.at[xm, k], g_send.at[0, k], g_recv.at[0, k], at(xp, y, z, c)).wait_recv()
        remote(b_ref.at[k], colbuf.at[xp, k], g_send.at[1, k], g_recv.at[1, k], at(xm, y, z, c)).wait_recv()
        remote(b_ref.at[k], rowbuf.at[ym, k], g_send.at[4, k], g_recv.at[4, k], at(x, yp, z, c)).wait_recv()
        remote(b_ref.at[k], rowbuf.at[yp, k], g_send.at[5, k], g_recv.at[5, k], at(x, ym, z, c)).wait_recv()

    xo, yo = up(x, 2, SIDE), up(y, 2, SIDE)

    def arrive_onward(k):
        remote(b_ref.at[k, lo], colbuf.at[xo, k, lo], g_send.at[2, k], g_recv.at[2, k], at(xp, y, z, c)).wait_recv()
        remote(b_ref.at[k, hi], colbuf.at[xo, k, hi], g_send.at[3, k], g_recv.at[3, k], at(xm, y, z, c)).wait_recv()
        remote(b_ref.at[k, lo], rowbuf.at[yo, k, lo], g_send.at[6, k], g_recv.at[6, k], at(x, yp, z, c)).wait_recv()
        remote(b_ref.at[k, hi], rowbuf.at[yo, k, hi], g_send.at[7, k], g_recv.at[7, k], at(x, ym, z, c)).wait_recv()

    for k in range(2):
        for copy in own(k):
            copy.start()

    colbuf[x] = b_ref[...]
    rowbuf[y] = b_ref[...]
    across = jnp.transpose(jnp.concatenate([rs_ref[...], jnp.zeros((2, R), F32)], axis=0))
    for k in range(KS):
        weight = prob_ref[assign_ref[k]] / SIDE_SCEN
        fac[k] = jnp.broadcast_to(across[:, k : k + 1] * weight, (R, T))
    acc[...] = jnp.zeros_like(acc)

    def contribute(k):
        who = assign_ref[k]
        left = []
        right = []
        for i in range(SIDE):
            row_on = pattern_ref[who, SIDE * x + i]
            col_on = pattern_ref[who, SIDE * i + y].astype(F32)
            tile = rowbuf[i, k]
            left.append(jnp.where(row_on != 0, tile, jnp.zeros_like(tile)))
            right.append((colbuf[i, k].astype(F32) * col_on * fac[k]).astype(BF16))
        left = jnp.concatenate(left, axis=1)
        right = jnp.concatenate(right, axis=1)
        acc[...] += lax.dot_general(left, right, (((0,), (0,)), ((), ())), preferred_element_type=F32)

    def step(k, carry):
        arrive_own(k)
        for copy in onward(k):
            copy.start()

        @pl.when(k < KS - 2)
        def _():
            for copy in own(k + 2):
                copy.start()

        @pl.when(k > 0)
        def _():
            arrive_onward(k - 1)
            contribute(k - 1)

        return carry

    lax.fori_loop(0, KS, step, 0)
    arrive_onward(KS - 1)
    contribute(KS - 1)

    rows = 2 * T
    swap = remote(
        acc.at[pl.ds(pl.multiple_of((1 - c) * rows, rows), rows)],
        core_in,
        c_send,
        c_recv,
        at(x, y, z, 1 - c),
    )
    swap.start()

    def drain(k, carry):
        for copy in own(k) + onward(k):
            copy.wait_send()
        return carry

    lax.fori_loop(0, KS, drain, 0)
    swap.wait_recv()
    first = pl.multiple_of(c * rows, rows)
    for j in range(NCHUNK):
        r0, c0 = (j // 4) * CROWS, (j % 4) * T
        part[j // 4, j % 4] = (
            acc[pl.ds(pl.multiple_of(first + r0, CROWS), CROWS), c0 : c0 + T] + core_in[r0 : r0 + CROWS, c0 : c0 + T]
        )

    m = lax.rem(z, 4)
    q = z // 4
    q01, q23 = pl.ds(0, 2), pl.ds(2, 2)

    def near_dev(by):
        return at(x, y, up(z, by, DEPTH), c)

    near = (
        remote(part.at[:, lax.rem(m + 1, 4)], near_in.at[0], na_send.at[0], na_recv.at[0], near_dev(1)),
        remote(part.at[:, lax.rem(m + 3, 4)], near_in.at[1], na_send.at[1], na_recv.at[1], near_dev(15)),
        remote(part.at[q01, lax.rem(m + 2, 4)], near_in.at[2, q01], na_send.at[2], na_recv.at[2], near_dev(2)),
        remote(part.at[q23, lax.rem(m + 2, 4)], near_in.at[2, q23], na_send.at[3], na_recv.at[3], near_dev(14)),
    )
    for copy in near:
        copy.start()
    for copy in near:
        copy.wait_recv()
    near_sum[...] = part[:, m] + near_in[0] + near_in[1] + near_in[2]
    far = tuple(
        remote(
            near_sum.at[up(q, s, 4)],
            far_in.at[s - 1],
            fa_send.at[s - 1],
            fa_recv.at[s - 1],
            near_dev(4 * s),
        )
        for s in (1, 2, 3)
    )
    for copy in far:
        copy.start()
    for copy in far:
        copy.wait_recv()
    total = near_sum[q] + far_in[0] + far_in[1] + far_in[2]
    on_diag = (2 * c + jl == y) & (jx == x)
    lane = lax.broadcasted_iota(jnp.int32, (CROWS, T), 1)
    row = lax.broadcasted_iota(jnp.int32, (CROWS, T), 0)
    diag = jnp.broadcast_to(fd_ref[pl.ds(SIDE * x + y, 1), :], (CROWS, T))
    spot = jnp.where(on_diag, row + CROWS * jh, -1)
    total = total + jnp.where(lane == spot, diag, 0.0)
    mine[...] = total
    block[q, m] = total

    place = remote(mine, own_block, o_send, o_recv, out_to)

    @pl.when(jnp.logical_not(stays))
    def _():
        place.start()

    @pl.when(stays)
    def _():
        own_block[...] = total

    spread = tuple(
        remote(mine, block.at[q, m], fb_send.at[s - 1], fb_recv.at[s - 1], near_dev(4 * s)) for s in (1, 2, 3)
    )
    for copy in spread:
        copy.start()
    for s in (1, 2, 3):
        remote(mine, block.at[up(q, 4 - s, 4), m], fb_send.at[s - 1], fb_recv.at[s - 1], near_dev(4 * s)).wait_recv()
    share = (
        remote(block.at[:, m], block.at[:, m], nb_send.at[0], nb_recv.at[0], near_dev(1)),
        remote(block.at[:, m], block.at[:, m], nb_send.at[1], nb_recv.at[1], near_dev(15)),
        remote(block.at[q01, m], block.at[q01, m], nb_send.at[2], nb_recv.at[2], near_dev(2)),
        remote(block.at[q23, m], block.at[q23, m], nb_send.at[3], nb_recv.at[3], near_dev(14)),
    )
    for copy in share:
        copy.start()
    m1, m2, m3 = lax.rem(m + 1, 4), lax.rem(m + 2, 4), lax.rem(m + 3, 4)
    remote(block.at[:, m], block.at[:, m3], nb_send.at[0], nb_recv.at[0], near_dev(1)).wait_recv()
    remote(block.at[:, m], block.at[:, m1], nb_send.at[1], nb_recv.at[1], near_dev(15)).wait_recv()
    remote(block.at[q01, m], block.at[q01, m2], nb_send.at[2], nb_recv.at[2], near_dev(2)).wait_recv()
    remote(block.at[q23, m], block.at[q23, m2], nb_send.at[3], nb_recv.at[3], near_dev(14)).wait_recv()

    def total_of(v):
        return jnp.sum(jnp.sum(jnp.sum(v, axis=0, keepdims=True), axis=1, keepdims=True), axis=2, keepdims=True)

    residual = rhs_ref[...]
    direction = residual
    answer = jnp.zeros_like(residual)
    norm_now = total_of(residual * residual)
    slot = 2 * x + c
    for it in range(ITERS):
        dvec[...] = direction
        for yl in range(2):
            halves = []
            for h in range(2):
                prod = None
                for xc in range(SIDE):
                    d = dvec[2 * xc + y // 2, pl.ds(lax.rem(y, 2), 1), :]
                    term = block[yl * 2 + h, xc] * d
                    prod = term if prod is None else prod + term
                halves.append(prod)
            both = jnp.concatenate(halves, axis=0)
            msg[it, pl.ds(yl, 1), :] = jnp.sum(jnp.transpose(both), axis=0, keepdims=True)

        def tell(i, carry):
            remote(msg.at[it], inbox.at[it, y, slot], m_send.at[it], m_recv.at[it], plane_peer(i)).start()
            return carry

        lax.fori_loop(1, 32, tell, 0)
        inbox[it, y, slot] = msg[it]
        pltpu.make_async_copy(tally, tally, m_recv.at[it]).wait()
        image = inbox[it, 0] + inbox[it, 1] + inbox[it, 2] + inbox[it, 3]
        alpha = norm_now / total_of(direction * image)
        answer = answer + alpha * direction
        if it < ITERS - 1:
            residual = residual - alpha * image
            norm_next = total_of(residual * residual)
            direction = residual + (norm_next / norm_now) * direction
            norm_now = norm_next
    sol_ref[...] = answer

    swap.wait_send()
    for copy in near + far + spread + share:
        copy.wait_send()
    for it in range(ITERS):
        pltpu.make_async_copy(tally, tally, m_send.at[it]).wait()

    @pl.when(jnp.logical_not(stays))
    def _():
        place.wait_send()
        place.wait_recv()

    schur_ref[...] = own_block[...]


SIDE_SCEN = 192


def on_device(borders, row_scale, assign, prob, pattern, first_diag, rhs):
    smem = pl.BlockSpec(memory_space=pltpu.SMEM)
    vmem = pl.BlockSpec(memory_space=pltpu.VMEM)
    dma = pltpu.SemaphoreType.DMA
    schur, answer = pl.pallas_call(
        kernel,
        out_shape=(
            jax.ShapeDtypeStruct((CROWS, T), F32),
            jax.ShapeDtypeStruct((8, 2, T), F32),
        ),
        in_specs=[smem, smem, smem, vmem, vmem, vmem, vmem],
        out_specs=(vmem, vmem),
        scratch_shapes=[
            pltpu.VMEM((SIDE, KS, R, T), BF16),
            pltpu.VMEM((SIDE, KS, R, T), BF16),
            pltpu.VMEM((KS, R, T), F32),
            pltpu.VMEM((SIDE * T, SIDE * T), F32),
            pltpu.VMEM((2 * T, SIDE * T), F32),
            pltpu.VMEM((4, 4, CROWS, T), F32),
            pltpu.VMEM((3, 4, CROWS, T), F32),
            pltpu.VMEM((4, CROWS, T), F32),
            pltpu.VMEM((3, CROWS, T), F32),
            pltpu.VMEM((CROWS, T), F32),
            pltpu.VMEM((CROWS, T), F32),
            pltpu.VMEM((4, 4, CROWS, T), F32),
            pltpu.VMEM((8, 2, T), F32),
            pltpu.VMEM((ITERS, 2, T), F32),
            pltpu.VMEM((ITERS, SIDE, 8, 2, T), F32),
            pltpu.VMEM((31, 2, T), F32),
            dma((8, KS)),
            dma((8, KS)),
            dma,
            dma,
            dma((4,)),
            dma((4,)),
            dma((3,)),
            dma((3,)),
            dma((3,)),
            dma((3,)),
            dma((4,)),
            dma((4,)),
            dma,
            dma,
            dma((ITERS,)),
            dma((ITERS,)),
        ],
        compiler_params=pltpu.CompilerParams(
            collective_id=0, has_side_effects=True, vmem_limit_bytes=48 * 1024 * 1024
        ),
    )(assign, prob, pattern, borders, row_scale, first_diag.reshape(16, T), rhs.reshape(8, 2, T))
    return schur, answer.reshape(2048)


def solution(mesh):
    placed = (P("scen", None, "grp"), P("scen", None), P("scen"), P(), P(), P(), P())
    return jax.shard_map(
        on_device, mesh=mesh, in_specs=placed, out_specs=(P("scen", "grp"), P()), check_vma=False
    )
```

time: 363 us -> 121 us (0.33)
  waiting for transfers between devices: 164 us -> 0 us
  blocking collectives: 132 us -> 0 us
  Pallas kernels: 0 us -> 117 us
  between operations: 25.8 us -> 0.72 us
  starting transfers between devices: 13.2 us -> 0 us
  matrix products: 12.1 us -> 0 us
  other arithmetic: 11.9 us -> 0 us
    all_to_all x10 -> x0, blocking collectives: 132 us -> none  [from_everyone(): return lax.all_to_all(copies, axis, split_axis=0, concat_axis=0, tiled=True)]
    pallas_call x0 -> x1, Pallas kernels: none -> 117 us  [on_device(): pl.pallas_call(kernel, out_shape=(jax.ShapeDtypeStruct((CROWS, T), F32),...]
    all_gather x1 -> x0, waiting for transfers between devices: 109 us -> none  [on_device(): lax.all_gather(masked, 'grp', axis=2, tiled=True)]
    all_to_all x1 -> x0, waiting for transfers between devices: 54.9 us -> none  [summed_on_arrival(): lax.all_to_all(blocks, axis, split_axis=0, concat_axis=0, tiled=True)]
    all_to_all x1 -> x0, starting transfers between devices: 13.2 us -> none  [summed_on_arrival(): lax.all_to_all(blocks, axis, split_axis=0, concat_axis=0, tiled=True)]
    dot_general x9 -> x0, matrix products: 12.1 us -> none  [the longest x1 9.2 us: on_device(): jnp.einsum('krm,krj->mj', lax.all_gather(masked, 'grp', axis=2, tiled=Tru...]
    dot_general x9 -> x0, other arithmetic: 5.73 us -> none  [the longest x5 3.17 us: on_device(): jnp.dot(direction, image, precision=lax.Precision.HIGHEST)]
  transfers between devices with their start and end apart: 2 -> 0, of which waited for: 2 -> 0; matrix products, arithmetic and copies ran while one was open for 1% -> 0% of each run, Pallas kernels for 0% -> 0%
where the time goes in v1:
time: 121 us
  Pallas kernels  117 us (97%)
  local copies, waits for them, and re-layouts  3.21 us (3%)
    pallas_call x1, Pallas kernels, on_device(): pl.pallas_call(kernel, out_shape=(jax.ShapeDtypeStruct((CROWS, T), F32),...  117 us
    unnamed x15, local copies, waits for them, and re-layouts  3.21 us

profile of v1, /device:TPU:1, one launch (start us, length us, event | category | flops | bytes accessed | tf_op | source)
XLA Modules:
  0.0 121.0 jit_solution(8863456995642014688)
XLA Ops:
  0.6 0.0 copy-start.1
  0.6 0.0 copy-start.2
  0.7 0.0 copy-start.3
  0.7 0.0 copy-start.4
  0.7 0.0 copy-start.5
  0.7 0.8 copy.9.pattern_ref
  1.5 0.0 copy-done.1
  1.5 0.0 copy-done.2
  1.5 0.0 copy-done.3
  1.6 0.0 copy-done.4
  1.6 0.0 copy-done.5
  1.6 0.0 copy-start
  1.6 1.1 copy-done
  2.7 117.1 %shard_map.86 = (f32[64,128]{1,0:T(8,128)S(1)}, f32[8,2,128]{2,1,0:T(2,128)S(1)}) custom-call(s32[6]{0:T(128)S(1)} %copy-done.5, f32[192]{0:T(256)S(1)} %copy-done.4, s32[192,16]{1,0:T(8,128)S(1)} %copy.9.pattern_ref, bf16[6,512,128]{2,1,0:T(8,128)(2,1)S(1)} %copy-done, f32[6,512]{1,0:T(8,128)S(1)} %copy-done.1, f32[16,128]{1,0:T(8,128)S(1)} %bitcast.3, ...), custom_call_target="tpu_custom_call" | custom-call | tf_op jit(solution)/shard_map/pallas_call | solution.py:349
  119.8 0.6 copy.12
  120.4 0.6 copy.13
Async XLA Ops:
  0.6 0.9 copy-start.1
  0.6 0.9 copy-start.2
  0.7 0.9 copy-start.3
  0.7 0.9 copy-start.4
  0.7 0.9 copy-start.5
  1.6 1.1 copy-start

commit v2 on v0

v2 whole, which is shorter than its diff:
```python
import jax
import jax.numpy as jnp
from jax import lax
from jax.experimental import pallas as pl
from jax.experimental.pallas import tpu as pltpu
from jax.sharding import PartitionSpec as P


ITERS = 5
SIDE = 4
DEPTH = 16
SCEN = 192
KS = 6
R = 512
T = 128
HALF = R // 2
SUB = 32
REL = (0, 1, 3, 2)
NEAR = 3
ORDER = [(0, 0), (0, 1), (0, 2), (1, 0), (1, 1), (1, 2), (2, 0), (2, 1)]
ORDER += [(2, 2), (0, 3), (1, 3), (2, 3), (3, 0), (3, 1), (3, 2), (3, 3)]
INDEX = {where: i for i, where in enumerate(ORDER)}
MESH = pl.DeviceIdType.MESH
F32 = jnp.float32
BF16 = jnp.bfloat16


def kernel(
    assign_hbm,
    prob_hbm,
    pattern_hbm,
    b_hbm,
    rs_hbm,
    fd_hbm,
    rhs_hbm,
    schur_ref,
    sol_ref,
    assign_ref,
    prob_ref,
    pattern_ref,
    rs_ref,
    fd_ref,
    rhs_ref,
    rowbuf,
    colbuf,
    lefts,
    rights,
    fac,
    pat,
    acc,
    core_in,
    part,
    near_in,
    near_sum,
    far_in,
    mine,
    block,
    out_block,
    dvec,
    msg,
    inbox,
    tally,
    in_sem,
    g_send,
    g_recv,
    c_send,
    c_recv,
    na_send,
    na_recv,
    fa_send,
    fa_recv,
    fb_send,
    fb_recv,
    nb_send,
    nb_recv,
    o_send,
    o_recv,
    m_send,
    m_recv,
):
    scen = lax.axis_index("scen")
    grp = lax.axis_index("grp")
    z = scen // 2
    c = lax.rem(scen, 2)
    x = grp // SIDE
    y = lax.rem(grp, SIDE)

    def at(xx, yy, zz, cc):
        return (2 * zz + cc, SIDE * xx + yy)

    def up(v, by, n):
        return lax.rem(v + by, n)

    def remote(src, dst, send, recv, dev):
        return pltpu.make_async_remote_copy(
            src_ref=src, dst_ref=dst, send_sem=send, recv_sem=recv, device_id=dev, device_id_type=MESH
        )

    fetch_tiles = (
        pltpu.make_async_copy(b_hbm, colbuf.at[0], in_sem.at[0]),
        pltpu.make_async_copy(b_hbm, rowbuf.at[0], in_sem.at[1]),
    )
    fetch_small = tuple(
        pltpu.make_async_copy(src, dst, in_sem.at[2 + i])
        for i, (src, dst) in enumerate(
            (
                (assign_hbm, assign_ref),
                (prob_hbm, prob_ref),
                (pattern_hbm, pattern_ref),
                (rs_hbm, rs_ref),
                (fd_hbm, fd_ref),
                (rhs_hbm, rhs_ref),
            )
        )
    )
    for copy in fetch_tiles + fetch_small:
        copy.start()

    xs = [x] + [up(x, by, SIDE) for by in (1, 2, 3)]
    ys = [y] + [up(y, by, SIDE) for by in (1, 2, 3)]
    far_first = sorted(((a, b) for a in range(4) for b in range(4)), key=lambda d: -(min(d[0], 4 - d[0]) + min(d[1], 4 - d[1])))
    plane = []
    for dx, dy in far_first:
        for cc in (c, 1 - c):
            if (dx, dy) != (0, 0) or cc is not c:
                plane.append(at(xs[dx], ys[dy], z, cc))
    deep = {by: at(x, y, up(z, by, DEPTH), c) for by in (1, 2, 4, 8, 12, 14, 15)}

    with jax.named_scope("entry"):
        barrier = pltpu.get_barrier_semaphore()
        for peer in plane + list(deep.values()):
            pl.semaphore_signal(barrier, inc=1, device_id=peer, device_id_type=MESH)
        pl.semaphore_wait(barrier, len(plane) + len(deep))
        for copy in fetch_tiles:
            copy.wait()

    x_next, x_prev, y_next, y_prev = at(xs[1], y, z, c), at(xs[3], y, z, c), at(x, ys[1], z, c), at(x, ys[3], z, c)
    lo, hi = pl.ds(0, HALF), pl.ds(HALF, HALF)

    def hop(buf, kind, src, dst, k, rows, dev):
        return remote(buf.at[src, k, rows], buf.at[dst, k, rows], g_send.at[kind, k], g_recv.at[kind, k], dev)

    every = pl.ds(0, R)

    def own(k):
        return (
            hop(colbuf, 0, 0, 2, k, every, x_next),
            hop(colbuf, 1, 0, 1, k, every, x_prev),
            hop(rowbuf, 2, 0, 2, k, every, y_next),
            hop(rowbuf, 3, 0, 1, k, every, y_prev),
        )

    def onward(k):
        return (
            hop(colbuf, 4, 2, 3, k, lo, x_next),
            hop(colbuf, 5, 1, 3, k, hi, x_prev),
            hop(rowbuf, 6, 2, 3, k, lo, y_next),
            hop(rowbuf, 7, 1, 3, k, hi, y_prev),
        )

    def send_own(k, carry):
        for copy in own(k):
            copy.start()
        return carry

    lax.fori_loop(0, KS, send_own, 0)

    with jax.named_scope("setup"):
        for copy in fetch_small:
            copy.wait()
        across = jnp.transpose(jnp.concatenate([rs_ref[...], jnp.zeros((2, R), F32)], axis=0))
        slots = lax.broadcasted_iota(jnp.int32, (1, SCEN), 1)
        present = pattern_ref[...].astype(F32)
        for k in range(KS):
            held = (slots == assign_ref[:, k : k + 1]).astype(F32)
            weight = jnp.sum(prob_ref[...] * held, axis=1, keepdims=True) / SCEN
            fac[k] = jnp.broadcast_to(across[:, k : k + 1] * weight, (R, T))
            pat[k] = jnp.broadcast_to(jnp.sum(present * held, axis=1, keepdims=True), (16, T))
        acc[...] = jnp.zeros_like(acc)

    def masked(p, k):
        keep = pat[k, pl.ds(SIDE * x + ys[REL[p]], 1), :].astype(BF16)
        return rowbuf[p, k] * keep

    def scaled(p, k):
        keep = pat[k, pl.ds(SIDE * xs[REL[p]] + y, 1), :]
        return (colbuf[p, k].astype(F32) * keep * fac[k]).astype(BF16)

    def product(left, right):
        return lax.dot_general(left, right, (((0,), (0,)), ((), ())), preferred_element_type=F32)

    def gain(value, rows, cols):
        for i, pr in enumerate(rows):
            for j, pc in enumerate(cols):
                for h in range(2):
                    for s in range(2):
                        r0 = T * i + 64 * h + SUB * s
                        acc[INDEX[pr, pc], h, s] += value[r0 : r0 + SUB, T * j : T * j + T]

    def step_a(k, carry):
        for copy in own(k):
            copy.wait_recv()
        for copy in onward(k):
            copy.start()
        for p in range(NEAR):
            lefts[k, :, T * p : T * p + T] = masked(p, k)
            rights[k, :, T * p : T * p + T] = scaled(p, k)
        gain(product(lefts[k], rights[k]), range(NEAR), range(NEAR))
        return carry

    def step_b(k, carry):
        for copy in onward(k):
            copy.wait_recv()
        left, right = masked(3, k), scaled(3, k)
        gain(product(left, jnp.concatenate([rights[k], right], axis=1)), (3,), range(4))
        gain(product(lefts[k], right), range(NEAR), (3,))
        return carry

    m = lax.rem(z, 4)
    q = z // 4
    ms = [m] + [up(m, by, 4) for by in (1, 2, 3)]
    qs = [q] + [up(q, by, 4) for by in (1, 2, 3)]
    front, back = pl.ds(0, 2), pl.ds(2, 2)

    def swap(w):
        tiles = pl.ds(8 * w, 8)
        return remote(acc.at[tiles, 1 - c], core_in.at[tiles], c_send.at[w], c_recv.at[w], at(x, y, z, 1 - c))

    def combine(w):
        swap(w).wait_recv()
        for i in range(8):
            for s in range(2):
                part[w, i // 2, 2 * (i % 2) + s] = acc[8 * w + i, c, s] + core_in[8 * w + i, s]

    def near(w):
        return (
            remote(part.at[w, :, ms[1]], near_in.at[w, 0], na_send.at[w, 0], na_recv.at[w, 0], deep[1]),
            remote(part.at[w, :, ms[3]], near_in.at[w, 1], na_send.at[w, 1], na_recv.at[w, 1], deep[15]),
            remote(part.at[w, front, ms[2]], near_in.at[w, 2, front], na_send.at[w, 2], na_recv.at[w, 2], deep[2]),
            remote(part.at[w, back, ms[2]], near_in.at[w, 2, back], na_send.at[w, 3], na_recv.at[w, 3], deep[14]),
        )

    def near_done(w):
        for copy in near(w):
            copy.wait_recv()
        near_sum[w] = part[w, :, m] + near_in[w, 0] + near_in[w, 1] + near_in[w, 2]

    def far(w):
        return tuple(
            remote(near_sum.at[w, qs[s]], far_in.at[w, s - 1], fa_send.at[w, s - 1], fa_recv.at[w, s - 1], deep[4 * s])
            for s in (1, 2, 3)
        )

    def far_done(w):
        for copy in far(w):
            copy.wait_recv()
        total = near_sum[w, q] + far_in[w, 0] + far_in[w, 1] + far_in[w, 2]
        if w == 0:
            lane = lax.broadcasted_iota(jnp.int32, (SUB, T), 1)
            row = lax.broadcasted_iota(jnp.int32, (SUB, T), 0)
            diag = jnp.broadcast_to(fd_ref[x, pl.ds(y, 1), :], (SUB, T))
            spot = jnp.where(z < 2, row + 64 * c + SUB * lax.rem(z, 2), -1)
            total = total + jnp.where(lane == spot, diag, 0.0)
        mine[w] = total
        block[w, q, m] = total

    def spread(w):
        return tuple(
            remote(mine.at[w], block.at[w, q, m], fb_send.at[w, s - 1], fb_recv.at[w, s - 1], deep[4 * s])
            for s in (1, 2, 3)
        )

    def share(w):
        return tuple(
            remote(block.at[w, sel, m], block.at[w, sel, m], nb_send.at[w, i], nb_recv.at[w, i], deep[by])
            for i, (sel, by) in enumerate(((pl.ds(0, 4), 1), (pl.ds(0, 4), 15), (front, 2), (back, 14)))
        )

    def start(copies):
        for copy in copies:
            copy.start()

    def wait_recv(copies):
        for copy in copies:
            copy.wait_recv()

    with jax.named_scope("gather_a"):
        lax.fori_loop(0, KS, step_a, 0)
    swap(0).start()
    with jax.named_scope("gather_b0"):
        lax.fori_loop(0, 2, step_b, 0)
    with jax.named_scope("swap_a"):
        combine(0)
    start(near(0))
    with jax.named_scope("gather_b1"):
        lax.fori_loop(2, KS, step_b, 0)
    swap(1).start()
    with jax.named_scope("near_a"):
        near_done(0)
    start(far(0))
    with jax.named_scope("swap_b"):
        combine(1)
    start(near(1))
    with jax.named_scope("near_b"):
        near_done(1)
    start(far(1))
    with jax.named_scope("far_a"):
        far_done(0)
    start(spread(0))
    with jax.named_scope("far_b"):
        far_done(1)
    start(spread(1))
    with jax.named_scope("spread_a"):
        wait_recv(spread(0))
    start(share(0))
    with jax.named_scope("spread_b"):
        wait_recv(spread(1))
    start(share(1))
    with jax.named_scope("share_ab"):
        wait_recv(share(0))
        wait_recv(share(1))

    def total_of(v):
        return jnp.sum(jnp.sum(jnp.sum(v, axis=0, keepdims=True), axis=1, keepdims=True), axis=2, keepdims=True)

    def tile_at(idx):
        return idx // 8, lax.rem(idx, 8) // 2, 2 * lax.rem(idx, 2)

    rel = lax.rem(m + SIDE - y, SIDE)
    out_row = jnp.where(rel == 2, 3, jnp.where(rel == 3, 2, rel))
    giver = x == q

    def out_tile(pc):
        idx = INDEX[0, pc]
        for pr in (1, 2, 3):
            idx = jnp.where(out_row == pr, INDEX[pr, pc], idx)
        return tile_at(idx)

    def give(pc):
        w, qq, mm = out_tile(pc)
        dev = at(xs[REL[pc]], y, z, c)
        return remote(block.at[w, qq, pl.ds(mm, 2)], out_block, o_send.at[pc - 1], o_recv, dev)

    residual = rhs_ref[...]
    direction = residual
    answer = jnp.zeros_like(residual)
    norm_now = total_of(residual * residual)
    for it in range(ITERS):
        with jax.named_scope(f"cg{it}"):
            dvec[...] = direction
            for pr in range(4):
                halves = []
                for s in range(2):
                    prod = None
                    for pc in range(4):
                        d = dvec[xs[REL[pc]], pl.ds(y, 1), :]
                        i = INDEX[pr, pc]
                        term = block[i // 8, (i % 8) // 2, 2 * (i % 2) + s] * d
                        prod = term if prod is None else prod + term
                    halves.append(prod)
                both = jnp.concatenate(halves, axis=0)
                placed = [jnp.where(c == h, both, jnp.zeros_like(both)) for h in range(2)]
                line = jnp.sum(jnp.transpose(jnp.concatenate(placed, axis=0)), axis=0, keepdims=True)
                msg[it, pl.ds(ys[REL[pr]], 1), :] = line
            for peer in plane:
                remote(msg.at[it], inbox.at[it, 2 * y + c, x], m_send.at[it], m_recv.at[it], peer).start()
            inbox[it, 2 * y + c, x] = msg[it]
            if it == ITERS - 1:

                @pl.when(giver)
                def _():
                    for pc in (1, 2, 3):
                        give(pc).start()
                    w, qq, mm = out_tile(0)
                    out_block[...] = block[w, qq, pl.ds(mm, 2)]

            pltpu.make_async_copy(tally, tally, m_recv.at[it]).wait()
            image = inbox[it, 0]
            for i in range(1, 8):
                image = image + inbox[it, i]
            alpha = norm_now / total_of(direction * image)
            answer = answer + alpha * direction
            if it < ITERS - 1:
                residual = residual - alpha * image
                norm_next = total_of(residual * residual)
                direction = residual + (norm_next / norm_now) * direction
                norm_now = norm_next
    sol_ref[...] = answer

    with jax.named_scope("finish"):

        @pl.when(jnp.logical_not(giver))
        def _():
            give(1).wait_recv()

        for s in range(2):
            schur_ref[SUB * s : SUB * s + SUB] = out_block[s]

        def drain(k, carry):
            for copy in own(k) + onward(k):
                copy.wait_send()
            return carry

        lax.fori_loop(0, KS, drain, 0)
        for w in range(2):
            swap(w).wait_send()
            for copy in near(w) + far(w) + spread(w) + share(w):
                copy.wait_send()
        for it in range(ITERS):
            pltpu.make_async_copy(tally, tally, m_send.at[it]).wait()

        @pl.when(giver)
        def _():
            for pc in (1, 2, 3):
                give(pc).wait_send()


def on_device(borders, row_scale, assign, prob, pattern, first_diag, rhs):
    held = pl.BlockSpec(memory_space=pltpu.HBM)
    vmem = pl.BlockSpec(memory_space=pltpu.VMEM)
    dma = pltpu.SemaphoreType.DMA
    schur, answer = pl.pallas_call(
        kernel,
        out_shape=(
            jax.ShapeDtypeStruct((2 * SUB, T), F32),
            jax.ShapeDtypeStruct((SIDE, SIDE, T), F32),
        ),
        in_specs=[held] * 7,
        out_specs=(vmem, vmem),
        scratch_shapes=[
            pltpu.VMEM((1, KS), jnp.int32),
            pltpu.VMEM((1, SCEN), F32),
            pltpu.VMEM((16, SCEN), jnp.int32),
            pltpu.VMEM((KS, R), F32),
            pltpu.VMEM((SIDE, SIDE, T), F32),
            pltpu.VMEM((SIDE, SIDE, T), F32),
            pltpu.VMEM((4, KS, R, T), BF16),
            pltpu.VMEM((4, KS, R, T), BF16),
            pltpu.VMEM((KS, R, NEAR * T), BF16),
            pltpu.VMEM((KS, R, NEAR * T), BF16),
            pltpu.VMEM((KS, R, T), F32),
            pltpu.VMEM((KS, 16, T), F32),
            pltpu.VMEM((16, 2, 2, SUB, T), F32),
            pltpu.VMEM((16, 2, SUB, T), F32),
            pltpu.VMEM((2, 4, 4, SUB, T), F32),
            pltpu.VMEM((2, 3, 4, SUB, T), F32),
            pltpu.VMEM((2, 4, SUB, T), F32),
            pltpu.VMEM((2, 3, SUB, T), F32),
            pltpu.VMEM((2, SUB, T), F32),
            pltpu.VMEM((2, 4, 4, SUB, T), F32),
            pltpu.VMEM((2, SUB, T), F32),
            pltpu.VMEM((SIDE, SIDE, T), F32),
            pltpu.VMEM((ITERS, SIDE, T), F32),
            pltpu.VMEM((ITERS, 8, SIDE, SIDE, T), F32),
            pltpu.VMEM((31, SIDE, T), F32),
            dma((8,)),
            dma((8, KS)),
            dma((8, KS)),
            dma((2,)),
            dma((2,)),
            dma((2, 4)),
            dma((2, 4)),
            dma((2, 3)),
            dma((2, 3)),
            dma((2, 3)),
            dma((2, 3)),
            dma((2, 4)),
            dma((2, 4)),
            dma((3,)),
            dma,
            dma((ITERS,)),
            dma((ITERS,)),
        ],
        compiler_params=pltpu.CompilerParams(
            collective_id=0, has_side_effects=True, vmem_limit_bytes=67_043_328
        ),
    )(
        assign.reshape(1, KS),
        prob.reshape(1, SCEN),
        pattern.T,
        borders,
        row_scale,
        first_diag.reshape(SIDE, SIDE, T),
        rhs.reshape(SIDE, SIDE, T),
    )
    return schur, answer.reshape(SIDE * SIDE * T)


def solution(mesh):
    placed = (P("scen", None, "grp"), P("scen", None), P("scen"), P(), P(), P(), P())
    return jax.shard_map(
        on_device, mesh=mesh, in_specs=placed, out_specs=(P("scen", "grp"), P()), check_vma=False
    )
```

time: 363 us -> 106 us (0.29)
  waiting for transfers between devices: 164 us -> 0 us
  blocking collectives: 132 us -> 0 us
  Pallas kernels: 0 us -> 103 us
  between operations: 25.8 us -> 0.65 us
  starting transfers between devices: 13.2 us -> 0 us
  matrix products: 12.1 us -> 0 us
  other arithmetic: 11.9 us -> 0 us
    all_to_all x10 -> x0, blocking collectives: 132 us -> none  [from_everyone(): return lax.all_to_all(copies, axis, split_axis=0, concat_axis=0, tiled=True)]
    all_gather x1 -> x0, waiting for transfers between devices: 109 us -> none  [on_device(): lax.all_gather(masked, 'grp', axis=2, tiled=True)]
    pallas_call x0 -> x1, Pallas kernels: none -> 103 us  [on_device(): pl.pallas_call(kernel, out_shape=(jax.ShapeDtypeStruct((2 * SUB, T), F32)...]
    all_to_all x1 -> x0, waiting for transfers between devices: 54.9 us -> none  [summed_on_arrival(): lax.all_to_all(blocks, axis, split_axis=0, concat_axis=0, tiled=True)]
    all_to_all x1 -> x0, starting transfers between devices: 13.2 us -> none  [summed_on_arrival(): lax.all_to_all(blocks, axis, split_axis=0, concat_axis=0, tiled=True)]
    dot_general x9 -> x0, matrix products: 12.1 us -> none  [the longest x1 9.2 us: on_device(): jnp.einsum('krm,krj->mj', lax.all_gather(masked, 'grp', axis=2, tiled=Tru...]
    dot_general x9 -> x0, other arithmetic: 5.73 us -> none  [the longest x5 3.17 us: on_device(): jnp.dot(direction, image, precision=lax.Precision.HIGHEST)]
  transfers between devices with their start and end apart: 2 -> 0, of which waited for: 2 -> 0; matrix products, arithmetic and copies ran while one was open for 1% -> 0% of each run, Pallas kernels for 0% -> 0%
where the time goes in v2:
time: 106 us
  Pallas kernels  103 us (97%)
  local copies, waits for them, and re-layouts  1.98 us (2%)
    pallas_call x1, Pallas kernels, on_device(): pl.pallas_call(kernel, out_shape=(jax.ShapeDtypeStruct((2 * SUB, T), F32)...  103 us

profile of v2, /device:TPU:1, one launch (start us, length us, event | category | flops | bytes accessed | tf_op | source)
XLA Modules:
  0.0 105.5 jit_solution(4870531600285081293)
XLA Ops:
  0.6 102.9 %shard_map.86 = (f32[64,128]{1,0:T(8,128)}, f32[4,4,128]{2,1,0:T(4,128)}) custom-call(s32[1,6]{1,0:T(1,128)} %bitcast.11, f32[1,192]{1,0:T(1,128)} %bitcast.10, s32[16,192]{1,0:T(8,128)} %bitcast.6, bf16[6,512,128]{2,1,0:T(8,128)(2,1)} %b_hbm.1, f32[6,512]{1,0:T(8,128)} %rs_hbm.1, f32[4,4,128]{2,1,0:T(4,128)} %bitcast.7, f32[4,4,128]{2,1,0:T(4,128)} %bitcast.8), custom_call_target="tpu_custom_call" | custom-call | tf_op jit(solution)/shard_map/pallas_call | solution.py:422
  103.5 0.0 copy-start
  103.5 1.4 %copy.11 = f32[64,128]{1,0:T(8,128)} copy(f32[64,128]{1,0:T(8,128)} %get-tuple-element.8) | data formatting | bytes 65536
  104.9 0.0 copy-done
  104.9 0.6 copy.12
Async XLA Ops:
  103.5 1.4 %copy-start = (f32[4,4,128]{2,1,0:T(4,128)S(1)}, f32[4,4,128]{2,1,0:T(4,128)}, u32[]{:S(2)}) copy-start(f32[4,4,128]{2,1,0:T(4,128)} %get-tuple-element.5) | copy-start | bytes 24580

commit v3 on v2

--- a/solution.py
+++ b/solution.py
@@ -7,6 +7,7 @@
 
 
 ITERS = 5
+EARLY = 2
 SIDE = 4
 DEPTH = 16
 SCEN = 192
@@ -59,6 +60,8 @@
     dvec,
     msg,
     inbox,
+    zmsg,
+    zbox,
     tally,
     in_sem,
     g_send,
@@ -77,6 +80,8 @@
     o_recv,
     m_send,
     m_recv,
+    z_send,
+    z_recv,
 ):
     scen = lax.axis_index("scen")
     grp = lax.axis_index("grp")
@@ -124,7 +129,7 @@
         for cc in (c, 1 - c):
             if (dx, dy) != (0, 0) or cc is not c:
                 plane.append(at(xs[dx], ys[dy], z, cc))
-    deep = {by: at(x, y, up(z, by, DEPTH), c) for by in (1, 2, 4, 8, 12, 14, 15)}
+    deep = {by: at(x, y, up(z, by, DEPTH), c) for by in range(1, DEPTH)}
 
     with jax.named_scope("entry"):
         barrier = pltpu.get_barrier_semaphore()
@@ -284,6 +289,72 @@
         for copy in copies:
             copy.wait_recv()
 
+    def total_of(v):
+        return jnp.sum(jnp.sum(jnp.sum(v, axis=0, keepdims=True), axis=1, keepdims=True), axis=2, keepdims=True)
+
+    def share_of(direction, tile, pieces):
+        dvec[...] = direction
+        lines = []
+        for pr in range(4):
+            stack = []
+            for piece in pieces:
+                prod = None
+                for pc in range(4):
+                    term = tile(INDEX[pr, pc], piece) * dvec[xs[REL[pc]], pl.ds(y, 1), :]
+                    prod = term if prod is None else prod + term
+                stack.append(prod)
+            both = jnp.concatenate(stack, axis=0)
+            if len(pieces) == 2:
+                both = jnp.concatenate([jnp.where(c == h, both, jnp.zeros_like(both)) for h in range(2)], axis=0)
+            lines.append(jnp.sum(jnp.transpose(both), axis=0, keepdims=True))
+        return lines
+
+    def write_lines(ref, it, lines):
+        for pr in range(4):
+            ref[it, pl.ds(ys[REL[pr]], 1), :] = lines[pr]
+
+    def tell(it):
+        for peer in plane:
+            remote(msg.at[it], inbox.at[it, 2 * y + c, x], m_send.at[it], m_recv.at[it], peer).start()
+        inbox[it, 2 * y + c, x] = msg[it]
+
+    def heard(it):
+        pltpu.make_async_copy(tally, tally, m_recv.at[it]).wait()
+        image = inbox[it, 0]
+        for i in range(1, 8):
+            image = image + inbox[it, i]
+        return image
+
+    deep_tally = tally.at[pl.ds(0, DEPTH - 1)]
+
+    def early_begin(it, state):
+        lines = share_of(state[2], lambda i, p: acc[i, p // 2, p % 2], range(4))
+        write_lines(zmsg, it, lines)
+        for by in (8, 7, 9, 6, 10, 5, 11, 4, 12, 3, 13, 2, 14, 1, 15):
+            remote(zmsg.at[it], zbox.at[it, z], z_send.at[it], z_recv.at[it], deep[by]).start()
+        zbox[it, z] = zmsg[it]
+
+    def early_middle(it):
+        pltpu.make_async_copy(deep_tally, deep_tally, z_recv.at[it]).wait()
+        total = zbox[it, 0]
+        for i in range(1, DEPTH):
+            total = total + zbox[it, i]
+        msg[it] = total
+        tell(it)
+
+    def update(it, state, image):
+        answer, residual, direction, norm_now = state
+        alpha = norm_now / total_of(direction * image)
+        answer = answer + alpha * direction
+        if it == ITERS - 1:
+            return answer, residual, direction, norm_now
+        residual = residual - alpha * image
+        norm_next = total_of(residual * residual)
+        return answer, residual, residual + (norm_next / norm_now) * direction, norm_next
+
+    def early_end(it, state):
+        return update(it, state, heard(it) + fd_ref[...] * state[2])
+
     with jax.named_scope("gather_a"):
         lax.fori_loop(0, KS, step_a, 0)
     swap(0).start()
@@ -295,6 +366,10 @@
     with jax.named_scope("gather_b1"):
         lax.fori_loop(2, KS, step_b, 0)
     swap(1).start()
+    with jax.named_scope("begin_0"):
+        rhs = rhs_ref[...]
+        state = (jnp.zeros_like(rhs), rhs, rhs, total_of(rhs * rhs))
+        early_begin(0, state)
     with jax.named_scope("near_a"):
         near_done(0)
     start(far(0))
@@ -304,24 +379,30 @@
     with jax.named_scope("near_b"):
         near_done(1)
     start(far(1))
+    with jax.named_scope("middle_0"):
+        early_middle(0)
     with jax.named_scope("far_a"):
         far_done(0)
     start(spread(0))
+    with jax.named_scope("end_0"):
+        state = early_end(0, state)
+        early_begin(1, state)
     with jax.named_scope("far_b"):
         far_done(1)
     start(spread(1))
     with jax.named_scope("spread_a"):
         wait_recv(spread(0))
     start(share(0))
+    with jax.named_scope("middle_1"):
+        early_middle(1)
     with jax.named_scope("spread_b"):
         wait_recv(spread(1))
     start(share(1))
+    with jax.named_scope("end_1"):
+        state = early_end(1, state)
     with jax.named_scope("share_ab"):
         wait_recv(share(0))
         wait_recv(share(1))
-
-    def total_of(v):
-        return jnp.sum(jnp.sum(jnp.sum(v, axis=0, keepdims=True), axis=1, keepdims=True), axis=2, keepdims=True)
 
     def tile_at(idx):
         return idx // 8, lax.rem(idx, 8) // 2, 2 * lax.rem(idx, 2)
@@ -341,30 +422,11 @@
         dev = at(xs[REL[pc]], y, z, c)
         return remote(block.at[w, qq, pl.ds(mm, 2)], out_block, o_send.at[pc - 1], o_recv, dev)
 
-    residual = rhs_ref[...]
-    direction = residual
-    answer = jnp.zeros_like(residual)
-    norm_now = total_of(residual * residual)
-    for it in range(ITERS):
+    for it in range(EARLY, ITERS):
         with jax.named_scope(f"cg{it}"):
-            dvec[...] = direction
-            for pr in range(4):
-                halves = []
-                for s in range(2):
-                    prod = None
-                    for pc in range(4):
-                        d = dvec[xs[REL[pc]], pl.ds(y, 1), :]
-                        i = INDEX[pr, pc]
-                        term = block[i // 8, (i % 8) // 2, 2 * (i % 2) + s] * d
-                        prod = term if prod is None else prod + term
-                    halves.append(prod)
-                both = jnp.concatenate(halves, axis=0)
-                placed = [jnp.where(c == h, both, jnp.zeros_like(both)) for h in range(2)]
-                line = jnp.sum(jnp.transpose(jnp.concatenate(placed, axis=0)), axis=0, keepdims=True)
-                msg[it, pl.ds(ys[REL[pr]], 1), :] = line
-            for peer in plane:
-                remote(msg.at[it], inbox.at[it, 2 * y + c, x], m_send.at[it], m_recv.at[it], peer).start()
-            inbox[it, 2 * y + c, x] = msg[it]
+            lines = share_of(state[2], lambda i, p: block[i // 8, (i % 8) // 2, 2 * (i % 2) + p], range(2))
+            write_lines(msg, it, lines)
+            tell(it)
             if it == ITERS - 1:
 
                 @pl.when(giver)
@@ -374,17 +436,8 @@
                     w, qq, mm = out_tile(0)
                     out_block[...] = block[w, qq, pl.ds(mm, 2)]
 
-            pltpu.make_async_copy(tally, tally, m_recv.at[it]).wait()
-            image = inbox[it, 0]
-            for i in range(1, 8):
-                image = image + inbox[it, i]
-            alpha = norm_now / total_of(direction * image)
-            answer = answer + alpha * direction
-            if it < ITERS - 1:
-                residual = residual - alpha * image
-                norm_next = total_of(residual * residual)
-                direction = residual + (norm_next / norm_now) * direction
-                norm_now = norm_next
+            state = update(it, state, heard(it))
+    answer = state[0]
     sol_ref[...] = answer
 
     with jax.named_scope("finish"):
@@ -408,6 +461,8 @@
                 copy.wait_send()
         for it in range(ITERS):
             pltpu.make_async_copy(tally, tally, m_send.at[it]).wait()
+        for it in range(EARLY):
+            pltpu.make_async_copy(deep_tally, deep_tally, z_send.at[it]).wait()
 
         @pl.when(giver)
         def _():
@@ -452,6 +507,8 @@
             pltpu.VMEM((SIDE, SIDE, T), F32),
             pltpu.VMEM((ITERS, SIDE, T), F32),
             pltpu.VMEM((ITERS, 8, SIDE, SIDE, T), F32),
+            pltpu.VMEM((EARLY, SIDE, T), F32),
+            pltpu.VMEM((EARLY, DEPTH, SIDE, T), F32),
             pltpu.VMEM((31, SIDE, T), F32),
             dma((8,)),
             dma((8, KS)),
@@ -470,6 +527,8 @@
             dma,
             dma((ITERS,)),
             dma((ITERS,)),
+            dma((EARLY,)),
+            dma((EARLY,)),
         ],
         compiler_params=pltpu.CompilerParams(
             collective_id=0, has_side_effects=True, vmem_limit_bytes=67_043_328

time: 106 us -> 97.8 us (0.923)
  Pallas kernels: 103 us -> 95 us
    pallas_call x1, Pallas kernels: 103 us -> 95 us  [on_device(): pl.pallas_call(kernel, out_shape=(jax.ShapeDtypeStruct((2 * SUB, T), F32)...]
where the time goes in v3:
time: 97.8 us; the launch traced here: 97.6 us
  Pallas kernels  95 us (97%)
  local copies, waits for them, and re-layouts  1.98 us (2%)
    pallas_call x1, Pallas kernels, on_device(): pl.pallas_call(kernel, out_shape=(jax.ShapeDtypeStruct((2 * SUB, T), F32)...  95 us
    unnamed x4, local copies, waits for them, and re-layouts  1.98 us

profile of v3, /device:TPU:1, one launch (start us, length us, event | category | flops | bytes accessed | tf_op | source)
XLA Modules:
  0.0 97.6 jit_solution(14667991446889356217)
XLA Ops:
  0.6 95.0 %shard_map.86 = (f32[64,128]{1,0:T(8,128)}, f32[4,4,128]{2,1,0:T(4,128)}) custom-call(s32[1,6]{1,0:T(1,128)} %bitcast.11, f32[1,192]{1,0:T(1,128)} %bitcast.10, s32[16,192]{1,0:T(8,128)} %bitcast.6, bf16[6,512,128]{2,1,0:T(8,128)(2,1)} %b_hbm.1, f32[6,512]{1,0:T(8,128)} %rs_hbm.1, f32[4,4,128]{2,1,0:T(4,128)} %bitcast.7, f32[4,4,128]{2,1,0:T(4,128)} %bitcast.8), custom_call_target="tpu_custom_call" | custom-call | tf_op jit(solution)/shard_map/pallas_call | solution.py:477
  95.6 0.0 copy-start
  95.7 1.4 %copy.11 = f32[64,128]{1,0:T(8,128)} copy(f32[64,128]{1,0:T(8,128)} %get-tuple-element.8) | data formatting | bytes 65536
  97.0 0.0 copy-done
  97.0 0.6 copy.12
Async XLA Ops:
  95.6 1.4 %copy-start = (f32[4,4,128]{2,1,0:T(4,128)S(1)}, f32[4,4,128]{2,1,0:T(4,128)}, u32[]{:S(2)}) copy-start(f32[4,4,128]{2,1,0:T(4,128)} %get-tuple-element.5) | copy-start | bytes 24580

commit v4 on v3

v4 whole, which is shorter than its diff:
```python
import jax
import jax.numpy as jnp
from jax import lax
from jax.experimental import pallas as pl
from jax.experimental.pallas import tpu as pltpu
from jax.sharding import PartitionSpec as P


ITERS = 5
EARLY = 2
SIDE = 4
DEPTH = 16
SCEN = 192
KS = 6
R = 512
T = 128
HALF = R // 2
PARTS = 8
EACH = 16 // PARTS
SUB = 8
REL = (0, 1, 3, 2)
NEAR = 3
ORDER = [(0, 0), (0, 1), (0, 2), (1, 0), (1, 1), (1, 2), (2, 0), (2, 1)]
ORDER += [(2, 2), (0, 3), (1, 3), (2, 3), (3, 0), (3, 1), (3, 2), (3, 3)]
INDEX = {where: i for i, where in enumerate(ORDER)}
MESH = pl.DeviceIdType.MESH
F32 = jnp.float32
BF16 = jnp.bfloat16


def kernel(
    assign_hbm,
    prob_hbm,
    pattern_hbm,
    b_hbm,
    rs_hbm,
    fd_hbm,
    rhs_hbm,
    schur_hbm,
    sol_hbm,
    assign_ref,
    prob_ref,
    pattern_ref,
    rs_ref,
    fd_ref,
    rhs_ref,
    rowbuf,
    colbuf,
    lefts,
    rights,
    fac,
    pat,
    acc,
    core_in,
    part,
    near_in,
    near_sum,
    far_in,
    mine,
    block,
    out_block,
    dvec,
    msg,
    inbox,
    zmsg,
    zbox,
    tally,
    in_sem,
    g_send,
    g_recv,
    c_send,
    c_recv,
    na_send,
    na_recv,
    fa_send,
    fa_recv,
    fb_send,
    fb_recv,
    nb_send,
    nb_recv,
    o_send,
    o_recv,
    m_send,
    m_recv,
    z_send,
    z_recv,
):
    scen = lax.axis_index("scen")
    grp = lax.axis_index("grp")
    z = scen // 2
    c = lax.rem(scen, 2)
    x = grp // SIDE
    y = lax.rem(grp, SIDE)

    def at(xx, yy, zz, cc):
        return (2 * zz + cc, SIDE * xx + yy)

    def up(v, by, n):
        return lax.rem(v + by, n)

    def remote(src, dst, send, recv, dev):
        return pltpu.make_async_remote_copy(
            src_ref=src, dst_ref=dst, send_sem=send, recv_sem=recv, device_id=dev, device_id_type=MESH
        )

    def landed(like, sem):
        pltpu.make_async_copy(like, like, sem).wait()

    fetch_tiles = tuple(pltpu.make_async_copy(b_hbm.at[k], colbuf.at[0, k], in_sem.at[k]) for k in range(KS))
    fetch_small = tuple(
        pltpu.make_async_copy(src, dst, in_sem.at[KS + i])
        for i, (src, dst) in enumerate(
            (
                (assign_hbm, assign_ref),
                (prob_hbm, prob_ref),
                (pattern_hbm, pattern_ref),
                (rs_hbm, rs_ref),
                (fd_hbm, fd_ref),
                (rhs_hbm, rhs_ref),
                (b_hbm, rowbuf.at[0]),
            )
        )
    )
    for copy in fetch_tiles + fetch_small:
        copy.start()

    xs = [x] + [up(x, by, SIDE) for by in (1, 2, 3)]
    ys = [y] + [up(y, by, SIDE) for by in (1, 2, 3)]
    far_first = sorted(((a, b) for a in range(4) for b in range(4)), key=lambda d: -(min(d[0], 4 - d[0]) + min(d[1], 4 - d[1])))
    plane = []
    for dx, dy in far_first:
        for cc in (c, 1 - c):
            if (dx, dy) != (0, 0) or cc is not c:
                plane.append(at(xs[dx], ys[dy], z, cc))
    deep = {by: at(x, y, up(z, by, DEPTH), c) for by in range(1, DEPTH)}

    with jax.named_scope("entry"):
        barrier = pltpu.get_barrier_semaphore()
        for peer in plane + list(deep.values()):
            pl.semaphore_signal(barrier, inc=1, device_id=peer, device_id_type=MESH)
        pl.semaphore_wait(barrier, len(plane) + len(deep))

    x_next, x_prev, y_next, y_prev = at(xs[1], y, z, c), at(xs[3], y, z, c), at(x, ys[1], z, c), at(x, ys[3], z, c)
    lo, hi = pl.ds(0, HALF), pl.ds(HALF, HALF)

    def hop(buf, kind, src, dst, k, rows, dev):
        return remote(buf.at[src, k, rows], buf.at[dst, k, rows], g_send.at[kind], g_recv.at[kind, k], dev)

    every = pl.ds(0, R)

    def own(k):
        return (
            hop(colbuf, 0, 0, 2, k, every, x_next),
            hop(colbuf, 0, 0, 1, k, every, x_prev),
            remote(colbuf.at[0, k], rowbuf.at[2, k], g_send.at[0], g_recv.at[0, k], y_next),
            remote(colbuf.at[0, k], rowbuf.at[1, k], g_send.at[0], g_recv.at[0, k], y_prev),
        )

    def onward(k):
        return (
            hop(colbuf, 1, 2, 3, k, lo, x_next),
            hop(colbuf, 1, 1, 3, k, hi, x_prev),
            hop(rowbuf, 1, 2, 3, k, lo, y_next),
            hop(rowbuf, 1, 1, 3, k, hi, y_prev),
        )

    for k in range(KS):
        fetch_tiles[k].wait()
        for copy in own(k):
            copy.start()

    with jax.named_scope("setup"):
        for copy in fetch_small:
            copy.wait()
        across = jnp.transpose(jnp.concatenate([rs_ref[...], jnp.zeros((2, R), F32)], axis=0))
        slots = lax.broadcasted_iota(jnp.int32, (1, SCEN), 1)
        present = pattern_ref[...].astype(F32)
        for k in range(KS):
            held = (slots == assign_ref[:, k : k + 1]).astype(F32)
            weight = jnp.sum(prob_ref[...] * held, axis=1, keepdims=True) / SCEN
            fac[k] = jnp.broadcast_to(across[:, k : k + 1] * weight, (R, T))
            pat[k] = jnp.broadcast_to(jnp.sum(present * held, axis=1, keepdims=True), (16, T))
        acc[...] = jnp.zeros_like(acc)

    def masked(p, k):
        keep = pat[k, pl.ds(SIDE * x + ys[REL[p]], 1), :].astype(BF16)
        return rowbuf[p, k] * keep

    def scaled(p, k):
        keep = pat[k, pl.ds(SIDE * xs[REL[p]] + y, 1), :]
        return (colbuf[p, k].astype(F32) * keep * fac[k]).astype(BF16)

    def product(left, right):
        return lax.dot_general(left, right, (((0,), (0,)), ((), ())), preferred_element_type=F32)

    def gain(value, rows, cols):
        for i, pr in enumerate(rows):
            for j, pc in enumerate(cols):
                for h in range(2):
                    for s in range(8):
                        r0 = T * i + 64 * h + SUB * s
                        acc[INDEX[pr, pc], h, s] += value[r0 : r0 + SUB, T * j : T * j + T]

    def step_a(k, carry):
        landed(colbuf.at[:, k], g_recv.at[0, k])
        for copy in onward(k):
            copy.start()
        for p in range(NEAR):
            lefts[k, :, T * p : T * p + T] = masked(p, k)
            rights[k, :, T * p : T * p + T] = scaled(p, k)
        gain(product(lefts[k], rights[k]), range(NEAR), range(NEAR))
        return carry

    def step_b(k, carry):
        landed(colbuf.at[pl.ds(0, 2), k], g_recv.at[1, k])
        left, right = masked(3, k), scaled(3, k)
        gain(product(left, jnp.concatenate([rights[k], right], axis=1)), (3,), range(4))
        gain(product(lefts[k], right), range(NEAR), (3,))
        return carry

    m = lax.rem(z, 4)
    q = z // 4
    ms = [m] + [up(m, by, 4) for by in (1, 2, 3)]
    qs = [q] + [up(q, by, 4) for by in (1, 2, 3)]
    front, back = pl.ds(0, 2), pl.ds(2, 2)

    def swap(w):
        tiles = pl.ds(EACH * w, EACH)
        return remote(acc.at[tiles, 1 - c], core_in.at[tiles], c_send, c_recv.at[w], at(x, y, z, 1 - c))

    def combine(w):
        swap(w).wait_recv()
        for i in range(4):
            tile, s = EACH * w + i // 2, pl.ds(4 * (i % 2), 4)
            part[w, i] = acc[tile, c, s] + core_in[tile, s]

    def near(w):
        return (
            remote(part.at[w, :, ms[1]], near_in.at[w, 0], na_send, na_recv.at[w], deep[1]),
            remote(part.at[w, :, ms[3]], near_in.at[w, 1], na_send, na_recv.at[w], deep[15]),
            remote(part.at[w, front, ms[2]], near_in.at[w, 2, front], na_send, na_recv.at[w], deep[2]),
            remote(part.at[w, back, ms[2]], near_in.at[w, 2, back], na_send, na_recv.at[w], deep[14]),
        )

    def near_done(w):
        landed(near_in.at[w], na_recv.at[w])
        near_sum[w] = part[w, :, m] + near_in[w, 0] + near_in[w, 1] + near_in[w, 2]

    def far(w):
        return tuple(
            remote(near_sum.at[w, qs[s]], far_in.at[w, s - 1], fa_send, fa_recv.at[w], deep[4 * s]) for s in (1, 2, 3)
        )

    def far_done(w):
        landed(far_in.at[w], fa_recv.at[w])
        total = near_sum[w, q] + far_in[w, 0] + far_in[w, 1] + far_in[w, 2]
        if w == 0:
            lane = lax.broadcasted_iota(jnp.int32, (SUB, T), 1)
            row = lax.broadcasted_iota(jnp.int32, (SUB, T), 0)
            diag = jnp.broadcast_to(fd_ref[x, pl.ds(y, 1), :], (SUB, T))
            spot = jnp.where(z < 8, row + 64 * c + SUB * z, -1)
            total = total + jnp.where(lane == spot, diag, 0.0)
        mine[w] = total
        block[w, q, m] = total

    def spread(w):
        return tuple(remote(mine.at[w], block.at[w, q, m], fb_send, fb_recv.at[w], deep[4 * s]) for s in (1, 2, 3))

    def share(w):
        return tuple(
            remote(block.at[w, sel, m], block.at[w, sel, m], nb_send, nb_recv.at[w], deep[by])
            for sel, by in ((pl.ds(0, 4), 1), (pl.ds(0, 4), 15), (front, 2), (back, 14))
        )

    def start(copies):
        for copy in copies:
            copy.start()

    def total_of(v):
        return jnp.sum(jnp.sum(jnp.sum(v, axis=0, keepdims=True), axis=1, keepdims=True), axis=2, keepdims=True)

    def share_of(direction, tile, pieces):
        dvec[...] = direction
        lines = []
        for pr in range(4):
            stack = []
            for piece in pieces:
                prod = None
                for pc in range(4):
                    term = tile(INDEX[pr, pc], piece) * dvec[xs[REL[pc]], pl.ds(y, 1), :]
                    prod = term if prod is None else prod + term
                stack.append(prod)
            both = jnp.concatenate(stack, axis=0)
            if len(pieces) == 8:
                both = jnp.concatenate([jnp.where(c == h, both, jnp.zeros_like(both)) for h in range(2)], axis=0)
            lines.append(jnp.sum(jnp.transpose(both), axis=0, keepdims=True))
        return lines

    def write_lines(ref, it, lines):
        for pr in range(4):
            ref[it, pl.ds(ys[REL[pr]], 1), :] = lines[pr]

    def tell(it):
        for peer in plane:
            remote(msg.at[it], inbox.at[it, 2 * y + c, x], m_send.at[it], m_recv.at[it], peer).start()
        inbox[it, 2 * y + c, x] = msg[it]

    def heard(it):
        landed(tally, m_recv.at[it])
        image = inbox[it, 0]
        for i in range(1, 8):
            image = image + inbox[it, i]
        return image

    deep_tally = tally.at[pl.ds(0, DEPTH - 1)]

    def early_begin(it, state):
        lines = share_of(state[2], lambda i, p: acc[i, p // 8, p % 8], range(16))
        write_lines(zmsg, it, lines)
        for by in (8, 7, 9, 6, 10, 5, 11, 4, 12, 3, 13, 2, 14, 1, 15):
            remote(zmsg.at[it], zbox.at[it, z], z_send.at[it], z_recv.at[it], deep[by]).start()
        zbox[it, z] = zmsg[it]

    def early_middle(it):
        landed(deep_tally, z_recv.at[it])
        total = zbox[it, 0]
        for i in range(1, DEPTH):
            total = total + zbox[it, i]
        msg[it] = total
        tell(it)

    def update(it, state, image):
        answer, residual, direction, norm_now = state
        alpha = norm_now / total_of(direction * image)
        answer = answer + alpha * direction
        if it == ITERS - 1:
            return answer, residual, direction, norm_now
        residual = residual - alpha * image
        norm_next = total_of(residual * residual)
        return answer, residual, residual + (norm_next / norm_now) * direction, norm_next

    def early_end(it, state):
        return update(it, state, heard(it) + fd_ref[...] * state[2])

    early, late = range(PARTS // 2), range(PARTS // 2, PARTS)
    with jax.named_scope("gather_a"):
        lax.fori_loop(0, KS, step_a, 0)
    for w in early:
        swap(w).start()
    with jax.named_scope("gather_b0"):
        lax.fori_loop(0, 1, step_b, 0)
    with jax.named_scope("swap_a"):
        for w in early:
            combine(w)
            start(near(w))
    with jax.named_scope("gather_b1"):
        lax.fori_loop(1, 4, step_b, 0)
    with jax.named_scope("near_a0"):
        for w in early[:2]:
            near_done(w)
            start(far(w))
    with jax.named_scope("gather_b2"):
        lax.fori_loop(4, 5, step_b, 0)
    with jax.named_scope("near_a1"):
        for w in early[2:]:
            near_done(w)
            start(far(w))
    with jax.named_scope("gather_b3"):
        lax.fori_loop(5, KS, step_b, 0)
    for w in late:
        swap(w).start()
    with jax.named_scope("begin_0"):
        rhs = rhs_ref[...]
        state = (jnp.zeros_like(rhs), rhs, rhs, total_of(rhs * rhs))
        early_begin(0, state)
    with jax.named_scope("swap_b"):
        for w in late:
            combine(w)
            start(near(w))
    with jax.named_scope("middle_0"):
        early_middle(0)
    with jax.named_scope("near_b"):
        for w in late:
            near_done(w)
            start(far(w))
    with jax.named_scope("far_a"):
        for w in early:
            far_done(w)
            start(spread(w))
    with jax.named_scope("end_0"):
        state = early_end(0, state)
        early_begin(1, state)
    with jax.named_scope("far_b"):
        for w in late:
            far_done(w)
            start(spread(w))
    with jax.named_scope("spread_a"):
        for w in early:
            landed(far_in.at[w], fb_recv.at[w])
            start(share(w))
    with jax.named_scope("middle_1"):
        early_middle(1)
    with jax.named_scope("spread_b"):
        for w in late:
            landed(far_in.at[w], fb_recv.at[w])
            start(share(w))
    with jax.named_scope("end_1"):
        state = early_end(1, state)
    with jax.named_scope("share_all"):
        for w in range(PARTS):
            landed(near_in.at[w], nb_recv.at[w])

    rel = lax.rem(m + SIDE - y, SIDE)
    out_row = jnp.where(rel == 2, 3, jnp.where(rel == 3, 2, rel))
    giver = x == q
    store_schur = pltpu.make_async_copy(out_block, schur_hbm, in_sem.at[0])
    store_answer = pltpu.make_async_copy(dvec, sol_hbm, in_sem.at[1])

    def out_tile(pc):
        idx = INDEX[0, pc]
        for pr in (1, 2, 3):
            idx = jnp.where(out_row == pr, INDEX[pr, pc], idx)
        return idx // EACH, pl.ds(2 * lax.rem(idx, EACH), 2)

    def give(pc):
        w, t = out_tile(pc)
        dev = at(xs[REL[pc]], y, z, c)
        return remote(block.at[w, t], out_block, o_send, o_recv, dev)

    for it in range(EARLY, ITERS):
        with jax.named_scope(f"cg{it}"):
            lines = share_of(state[2], lambda i, p: block[i // 2, 2 * (i % 2) + p // 4, p % 4], range(8))
            write_lines(msg, it, lines)
            tell(it)
            if it == ITERS - 1:

                @pl.when(giver)
                def _():
                    for pc in (1, 2, 3):
                        give(pc).start()
                    w, t = out_tile(0)
                    out_block[...] = block[w, t]


                @pl.when(jnp.logical_not(giver))
                def _():
                    give(1).wait_recv()

                store_schur.start()
            state = update(it, state, heard(it))
    dvec[...] = state[0]
    store_answer.start()

    with jax.named_scope("finish"):
        landed(colbuf, g_send.at[0])
        landed(colbuf.at[pl.ds(0, 2)], g_send.at[1])
        landed(core_in, c_send)
        landed(near_in, na_send)
        landed(far_in, fa_send)
        landed(far_in, fb_send)
        landed(near_in, nb_send)
        for it in range(ITERS):
            landed(tally, m_send.at[it])
        for it in range(EARLY):
            landed(deep_tally, z_send.at[it])

        @pl.when(giver)
        def _():
            landed(near_in.at[pl.ds(0, 2)], o_send)

        store_schur.wait()
        store_answer.wait()


def on_device(borders, row_scale, assign, prob, pattern, first_diag, rhs):
    held = pl.BlockSpec(memory_space=pltpu.HBM)
    dma = pltpu.SemaphoreType.DMA
    schur, answer = pl.pallas_call(
        kernel,
        out_shape=(
            jax.ShapeDtypeStruct((2, 4, SUB, T), F32),
            jax.ShapeDtypeStruct((SIDE, SIDE, T), F32),
        ),
        in_specs=[held] * 7,
        out_specs=(held, held),
        scratch_shapes=[
            pltpu.VMEM((1, KS), jnp.int32),
            pltpu.VMEM((1, SCEN), F32),
            pltpu.VMEM((16, SCEN), jnp.int32),
            pltpu.VMEM((KS, R), F32),
            pltpu.VMEM((SIDE, SIDE, T), F32),
            pltpu.VMEM((SIDE, SIDE, T), F32),
            pltpu.VMEM((4, KS, R, T), BF16),
            pltpu.VMEM((4, KS, R, T), BF16),
            pltpu.VMEM((KS, R, NEAR * T), BF16),
            pltpu.VMEM((KS, R, NEAR * T), BF16),
            pltpu.VMEM((KS, R, T), F32),
            pltpu.VMEM((KS, 16, T), F32),
            pltpu.VMEM((16, 2, 8, SUB, T), F32),
            pltpu.VMEM((16, 8, SUB, T), F32),
            pltpu.VMEM((PARTS, 4, 4, SUB, T), F32),
            pltpu.VMEM((PARTS, 3, 4, SUB, T), F32),
            pltpu.VMEM((PARTS, 4, SUB, T), F32),
            pltpu.VMEM((PARTS, 3, SUB, T), F32),
            pltpu.VMEM((PARTS, SUB, T), F32),
            pltpu.VMEM((PARTS, 4, 4, SUB, T), F32),
            pltpu.VMEM((2, 4, SUB, T), F32),
            pltpu.VMEM((SIDE, SIDE, T), F32),
            pltpu.VMEM((ITERS, SIDE, T), F32),
            pltpu.VMEM((ITERS, 8, SIDE, SIDE, T), F32),
            pltpu.VMEM((EARLY, SIDE, T), F32),
            pltpu.VMEM((EARLY, DEPTH, SIDE, T), F32),
            pltpu.VMEM((31, SIDE, T), F32),
            dma((KS + 7,)),
            dma((2,)),
            dma((2, KS)),
            dma,
            dma((PARTS,)),
            dma,
            dma((PARTS,)),
            dma,
            dma((PARTS,)),
            dma,
            dma((PARTS,)),
            dma,
            dma((PARTS,)),
            dma,
            dma,
            dma((ITERS,)),
            dma((ITERS,)),
            dma((EARLY,)),
            dma((EARLY,)),
        ],
        compiler_params=pltpu.CompilerParams(
            collective_id=0, has_side_effects=True, vmem_limit_bytes=67_043_328
        ),
    )(
        assign.reshape(1, KS),
        prob.reshape(1, SCEN),
        pattern.T,
        borders,
        row_scale,
        first_diag.reshape(SIDE, SIDE, T),
        rhs.reshape(SIDE, SIDE, T),
    )
    return schur.reshape(8 * SUB, T), answer.reshape(SIDE * SIDE * T)


def solution(mesh):
    placed = (P("scen", None, "grp"), P("scen", None), P("scen"), P(), P(), P(), P())
    return jax.shard_map(
        on_device, mesh=mesh, in_specs=placed, out_specs=(P("scen", "grp"), P()), check_vma=False
    )
```

time: 97.8 us -> 92.1 us (0.942)
  Pallas kernels: 95 us -> 89.3 us
    pallas_call x1, Pallas kernels: 95 us -> 89.3 us  [on_device(): pl.pallas_call(kernel, out_shape=(jax.ShapeDtypeStruct((2, 4, SUB, T), F3...]
where the time goes in v4:
time: 92.1 us; the launch traced here: 91.9 us
  Pallas kernels  89.3 us (97%)
  local copies, waits for them, and re-layouts  1.98 us (2%)
    pallas_call x1, Pallas kernels, on_device(): pl.pallas_call(kernel, out_shape=(jax.ShapeDtypeStruct((2, 4, SUB, T), F3...  89.3 us
    unnamed x4, local copies, waits for them, and re-layouts  1.98 us

profile of v4, /device:TPU:1, one launch (start us, length us, event | category | flops | bytes accessed | tf_op | source)
XLA Modules:
  0.0 91.9 jit_solution(10637122913401762297)
XLA Ops:
  0.6 89.3 %shard_map.86 = (f32[2,4,8,128]{3,2,1,0:T(8,128)}, f32[4,4,128]{2,1,0:T(4,128)}) custom-call(s32[1,6]{1,0:T(1,128)} %bitcast.13, f32[1,192]{1,0:T(1,128)} %bitcast.12, s32[16,192]{1,0:T(8,128)} %bitcast.8, bf16[6,512,128]{2,1,0:T(8,128)(2,1)} %b_hbm.1, f32[6,512]{1,0:T(8,128)} %rs_hbm.1, f32[4,4,128]{2,1,0:T(4,128)} %bitcast.9, f32[4,4,128]{2,1,0:T(4,128)} %bitcast.10), custom_call_target="tpu_custom_call" | custom-call | tf_op jit(solution)/shard_map/pallas_call | solution.py:478
  89.9 0.0 copy-start
  90.0 1.4 %copy.11 = f32[64,128]{1,0:T(8,128)} copy(f32[64,128]{1,0:T(8,128)} %bitcast.7) | data formatting | bytes 65536
  91.3 0.0 copy-done
  91.3 0.6 copy.12
Async XLA Ops:
  89.9 1.4 %copy-start = (f32[4,4,128]{2,1,0:T(4,128)S(1)}, f32[4,4,128]{2,1,0:T(4,128)}, u32[]{:S(2)}) copy-start(f32[4,4,128]{2,1,0:T(4,128)} %get-tuple-element.5) | copy-start | bytes 24580

commit v5 on v4

--- a/solution.py
+++ b/solution.py
@@ -36,8 +36,7 @@
     rs_hbm,
     fd_hbm,
     rhs_hbm,
-    schur_hbm,
-    sol_hbm,
+    out_hbm,
     assign_ref,
     prob_ref,
     pattern_ref,
@@ -59,6 +58,7 @@
     mine,
     block,
     out_block,
+    final,
     dvec,
     msg,
     inbox,
@@ -84,6 +84,7 @@
     m_recv,
     z_send,
     z_recv,
+    present_sem,
 ):
     scen = lax.axis_index("scen")
     grp = lax.axis_index("grp")
@@ -121,9 +122,6 @@
             )
         )
     )
-    for copy in fetch_tiles + fetch_small:
-        copy.start()
-
     xs = [x] + [up(x, by, SIDE) for by in (1, 2, 3)]
     ys = [y] + [up(y, by, SIDE) for by in (1, 2, 3)]
     far_first = sorted(((a, b) for a in range(4) for b in range(4)), key=lambda d: -(min(d[0], 4 - d[0]) + min(d[1], 4 - d[1])))
@@ -136,9 +134,12 @@
 
     with jax.named_scope("entry"):
         barrier = pltpu.get_barrier_semaphore()
-        for peer in plane + list(deep.values()):
+        first = plane + [deep[by] for by in (1, 2, 14, 15)]
+        for peer in first:
             pl.semaphore_signal(barrier, inc=1, device_id=peer, device_id_type=MESH)
-        pl.semaphore_wait(barrier, len(plane) + len(deep))
+        for copy in fetch_tiles + fetch_small:
+            copy.start()
+        pl.semaphore_wait(barrier, len(first))
 
     x_next, x_prev, y_next, y_prev = at(xs[1], y, z, c), at(xs[3], y, z, c), at(x, ys[1], z, c), at(x, ys[3], z, c)
     lo, hi = pl.ds(0, HALF), pl.ds(HALF, HALF)
@@ -168,6 +169,15 @@
         fetch_tiles[k].wait()
         for copy in own(k):
             copy.start()
+
+    def vouch(turn, by):
+        for peer in (deep[by], deep[DEPTH - by]):
+            pl.semaphore_signal(present_sem.at[turn], inc=1, device_id=peer, device_id_type=MESH)
+
+    def vouched(turn):
+        pl.semaphore_wait(present_sem.at[turn], 2)
+
+    vouch(0, 2)
 
     with jax.named_scope("setup"):
         for copy in fetch_small:
@@ -344,7 +354,11 @@
 
     early, late = range(PARTS // 2), range(PARTS // 2, PARTS)
     with jax.named_scope("gather_a"):
-        lax.fori_loop(0, KS, step_a, 0)
+        lax.fori_loop(0, 2, step_a, 0)
+        vouched(0)
+        vouch(1, 4)
+        lax.fori_loop(2, KS, step_a, 0)
+        vouched(1)
     for w in early:
         swap(w).start()
     with jax.named_scope("gather_b0"):
@@ -413,8 +427,10 @@
     rel = lax.rem(m + SIDE - y, SIDE)
     out_row = jnp.where(rel == 2, 3, jnp.where(rel == 3, 2, rel))
     giver = x == q
-    store_schur = pltpu.make_async_copy(out_block, schur_hbm, in_sem.at[0])
-    store_answer = pltpu.make_async_copy(dvec, sol_hbm, in_sem.at[1])
+    store_schur = tuple(
+        pltpu.make_async_copy(out_block.at[i], out_hbm.at[pl.ds(4 * i, 4)], in_sem.at[i]) for i in range(2)
+    )
+    store_answer = pltpu.make_async_copy(final, out_hbm.at[pl.ds(8, 2)], in_sem.at[2])
 
     def out_tile(pc):
         idx = INDEX[0, pc]
@@ -446,9 +462,10 @@
                 def _():
                     give(1).wait_recv()
 
-                store_schur.start()
+                start(store_schur)
             state = update(it, state, heard(it))
-    dvec[...] = state[0]
+    for i in range(SIDE):
+        final[i // 2, 4 * (i % 2) : 4 * (i % 2) + 4] = state[0][i]
     store_answer.start()
 
     with jax.named_scope("finish"):
@@ -468,21 +485,18 @@
         def _():
             landed(near_in.at[pl.ds(0, 2)], o_send)
 
-        store_schur.wait()
-        store_answer.wait()
+        for copy in store_schur + (store_answer,):
+            copy.wait()
 
 
 def on_device(borders, row_scale, assign, prob, pattern, first_diag, rhs):
     held = pl.BlockSpec(memory_space=pltpu.HBM)
     dma = pltpu.SemaphoreType.DMA
-    schur, answer = pl.pallas_call(
+    out = pl.pallas_call(
         kernel,
-        out_shape=(
-            jax.ShapeDtypeStruct((2, 4, SUB, T), F32),
-            jax.ShapeDtypeStruct((SIDE, SIDE, T), F32),
-        ),
+        out_shape=jax.ShapeDtypeStruct((10, 8, T), F32),
         in_specs=[held] * 7,
-        out_specs=(held, held),
+        out_specs=held,
         scratch_shapes=[
             pltpu.VMEM((1, KS), jnp.int32),
             pltpu.VMEM((1, SCEN), F32),
@@ -505,6 +519,7 @@
             pltpu.VMEM((PARTS, SUB, T), F32),
             pltpu.VMEM((PARTS, 4, 4, SUB, T), F32),
             pltpu.VMEM((2, 4, SUB, T), F32),
+            pltpu.VMEM((2, 8, T), F32),
             pltpu.VMEM((SIDE, SIDE, T), F32),
             pltpu.VMEM((ITERS, SIDE, T), F32),
             pltpu.VMEM((ITERS, 8, SIDE, SIDE, T), F32),
@@ -530,6 +545,7 @@
             dma((ITERS,)),
             dma((EARLY,)),
             dma((EARLY,)),
+            pltpu.SemaphoreType.REGULAR((2,)),
         ],
         compiler_params=pltpu.CompilerParams(
             collective_id=0, has_side_effects=True, vmem_limit_bytes=67_043_328
@@ -543,7 +559,7 @@
         first_diag.reshape(SIDE, SIDE, T),
         rhs.reshape(SIDE, SIDE, T),
     )
-    return schur.reshape(8 * SUB, T), answer.reshape(SIDE * SIDE * T)
+    return out[:8].reshape(8 * SUB, T), out[8:].reshape(SIDE * SIDE * T)
 
 
 def solution(mesh):

time: 92.1 us -> 91.4 us (level)
  Pallas kernels: 89.3 us -> 87.9 us
    reshape x0 -> x2, local copies, waits for them, and re-layouts: none -> 2.67 us  [on_device(): return (out[:8].reshape(8 * SUB, T), out[8:].reshape(SIDE * SIDE * T))]
    unnamed x4 -> x0, local copies, waits for them, and re-layouts: 1.98 us -> none
    pallas_call x1, Pallas kernels: 89.3 us -> 87.9 us  [on_device(): pl.pallas_call(kernel, out_shape=jax.ShapeDtypeStruct((10, 8, T), F32), i...]
where the time goes in v5:
time: 91.4 us; the launch traced here: 91.2 us
  Pallas kernels  87.9 us (96%)
  local copies, waits for them, and re-layouts  2.67 us (3%)
    pallas_call x1, Pallas kernels, on_device(): pl.pallas_call(kernel, out_shape=jax.ShapeDtypeStruct((10, 8, T), F32), i...  87.9 us
    reshape x2, local copies, waits for them, and re-layouts, on_device(): return (out[:8].reshape(8 * SUB, T), out[8:].reshape(SIDE * SIDE * T))  2.67 us

profile of v5, /device:TPU:1, one launch (start us, length us, event | category | flops | bytes accessed | tf_op | source)
XLA Modules:
  0.0 91.2 jit_solution(3927461365849768115)
XLA Ops:
  0.6 87.9 %shard_map.86 = f32[10,8,128]{2,1,0:T(8,128)} custom-call(s32[1,6]{1,0:T(1,128)} %bitcast.13, f32[1,192]{1,0:T(1,128)} %bitcast.12, s32[16,192]{1,0:T(8,128)} %bitcast.9, bf16[6,512,128]{2,1,0:T(8,128)(2,1)} %b_hbm.1, f32[6,512]{1,0:T(8,128)} %rs_hbm.1, f32[4,4,128]{2,1,0:T(4,128)} %bitcast.10, f32[4,4,128]{2,1,0:T(4,128)} %bitcast.11), custom_call_target="tpu_custom_call" | custom-call | tf_op jit(solution)/shard_map/pallas_call | solution.py:495
  88.5 1.3 %slice_bitcast_fusion.1 = f32[2048]{0:T(1024)} fusion(f32[10,8,128]{2,1,0:T(8,128)} %shard_map.86), kind=kLoop, calls=%fused_computation.1 | loop fusion | bytes 16384 | tf_op jit(solution)/shard_map/reshape | solution.py:562
  89.8 1.4 %slice_bitcast_fusion = f32[64,128]{1,0:T(8,128)} fusion(f32[10,8,128]{2,1,0:T(8,128)} %shard_map.86), kind=kLoop, calls=%fused_computation | loop fusion | bytes 65536 | tf_op jit(solution)/shard_map/reshape | solution.py:562

commit v6 on v5

--- a/solution.py
+++ b/solution.py
@@ -65,6 +65,10 @@
     zmsg,
     zbox,
     tally,
+    halves,
+    msg_half,
+    inbox_half,
+    tally_half,
     in_sem,
     g_send,
     g_recv,
@@ -132,9 +136,11 @@
                 plane.append(at(xs[dx], ys[dy], z, cc))
     deep = {by: at(x, y, up(z, by, DEPTH), c) for by in range(1, DEPTH)}
 
+    ring = [at(xs[1], y, z, c), at(xs[3], y, z, c), at(x, ys[1], z, c), at(x, ys[3], z, c)]
+
     with jax.named_scope("entry"):
         barrier = pltpu.get_barrier_semaphore()
-        first = plane + [deep[by] for by in (1, 2, 14, 15)]
+        first = ring + [at(x, y, z, 1 - c), deep[1], deep[15]]
         for peer in first:
             pl.semaphore_signal(barrier, inc=1, device_id=peer, device_id_type=MESH)
         for copy in fetch_tiles + fetch_small:
@@ -170,14 +176,20 @@
         for copy in own(k):
             copy.start()
 
-    def vouch(turn, by):
-        for peer in (deep[by], deep[DEPTH - by]):
-            pl.semaphore_signal(present_sem.at[turn], inc=1, device_id=peer, device_id_type=MESH)
+    def vouch(turn):
+        peers = list(ring)
+        if turn < 3:
+            peers += [deep[2**turn], deep[DEPTH - 2**turn]]
+        for i, peer in enumerate(peers):
+            sem = present_sem.at[turn] if i < 4 else present_sem.at[4 + turn]
+            pl.semaphore_signal(sem, inc=1, device_id=peer, device_id_type=MESH)
 
     def vouched(turn):
-        pl.semaphore_wait(present_sem.at[turn], 2)
-
-    vouch(0, 2)
+        pl.semaphore_wait(present_sem.at[turn], 4)
+        if turn < 3:
+            pl.semaphore_wait(present_sem.at[4 + turn], 2)
+
+    vouch(0)
 
     with jax.named_scope("setup"):
         for copy in fetch_small:
@@ -219,6 +231,14 @@
             lefts[k, :, T * p : T * p + T] = masked(p, k)
             rights[k, :, T * p : T * p + T] = scaled(p, k)
         gain(product(lefts[k], rights[k]), range(NEAR), range(NEAR))
+        for turn in range(4):
+
+            @pl.when(k == turn + 1)
+            def _():
+                vouched(turn)
+                if turn < 3:
+                    vouch(turn + 1)
+
         return carry
 
     def step_b(k, carry):
@@ -287,22 +307,24 @@
             copy.start()
 
     def total_of(v):
-        return jnp.sum(jnp.sum(jnp.sum(v, axis=0, keepdims=True), axis=1, keepdims=True), axis=2, keepdims=True)
-
-    def share_of(direction, tile, pieces):
-        dvec[...] = direction
+        for axis in range(v.ndim):
+            v = jnp.sum(v, axis=axis, keepdims=True)
+        return v
+
+    def share_of(tile, pieces, d_row):
         lines = []
         for pr in range(4):
             stack = []
             for piece in pieces:
                 prod = None
                 for pc in range(4):
-                    term = tile(INDEX[pr, pc], piece) * dvec[xs[REL[pc]], pl.ds(y, 1), :]
+                    term = tile(INDEX[pr, pc], piece) * d_row(xs[REL[pc]])
                     prod = term if prod is None else prod + term
                 stack.append(prod)
             both = jnp.concatenate(stack, axis=0)
             if len(pieces) == 8:
-                both = jnp.concatenate([jnp.where(c == h, both, jnp.zeros_like(both)) for h in range(2)], axis=0)
+                odd = lax.rem(ys[REL[pr]], 2)
+                both = jnp.concatenate([jnp.where(odd == h, both, jnp.zeros_like(both)) for h in range(2)], axis=0)
             lines.append(jnp.sum(jnp.transpose(both), axis=0, keepdims=True))
         return lines
 
@@ -325,7 +347,8 @@
     deep_tally = tally.at[pl.ds(0, DEPTH - 1)]
 
     def early_begin(it, state):
-        lines = share_of(state[2], lambda i, p: acc[i, p // 8, p % 8], range(16))
+        dvec[...] = state[2]
+        lines = share_of(lambda i, p: acc[i, p // 8, p % 8], range(16), lambda xx: dvec[xx, pl.ds(y, 1), :])
         write_lines(zmsg, it, lines)
         for by in (8, 7, 9, 6, 10, 5, 11, 4, 12, 3, 13, 2, 14, 1, 15):
             remote(zmsg.at[it], zbox.at[it, z], z_send.at[it], z_recv.at[it], deep[by]).start()
@@ -354,11 +377,7 @@
 
     early, late = range(PARTS // 2), range(PARTS // 2, PARTS)
     with jax.named_scope("gather_a"):
-        lax.fori_loop(0, 2, step_a, 0)
-        vouched(0)
-        vouch(1, 4)
-        lax.fori_loop(2, KS, step_a, 0)
-        vouched(1)
+        lax.fori_loop(0, KS, step_a, 0)
     for w in early:
         swap(w).start()
     with jax.named_scope("gather_b0"):
@@ -443,11 +462,40 @@
         dev = at(xs[REL[pc]], y, z, c)
         return remote(block.at[w, t], out_block, o_send, o_recv, dev)
 
-    for it in range(EARLY, ITERS):
+    def split(v):
+        for p in range(2):
+            for i in range(2):
+                halves[p, :, i : i + 1, :] = v[:, 2 * i + p : 2 * i + p + 1, :]
+        return halves[...]
+
+    low = lax.broadcasted_iota(jnp.int32, (SIDE, 2, T), 2) < 64
+
+    def heard_halves(n, it):
+        landed(tally_half, m_recv.at[it])
+        ours = []
+        for cc in range(2):
+            total = inbox_half[n, cc]
+            for i in range(1, SIDE):
+                total = total + inbox_half[n, 2 * i + cc]
+            ours.append(total)
+        turned = [pltpu.roll(v, 64, axis=2) for v in ours]
+        return jnp.stack([jnp.where(low, ours[0], turned[1]), jnp.where(low, turned[0], ours[1])])
+
+    state = tuple(split(v) for v in state[:3]) + (state[3].reshape(1, 1, 1, 1),)
+    for n, it in enumerate(range(EARLY, ITERS)):
         with jax.named_scope(f"cg{it}"):
-            lines = share_of(state[2], lambda i, p: block[i // 2, 2 * (i % 2) + p // 4, p % 4], range(8))
+            halves[...] = state[2]
+            lines = share_of(
+                lambda i, p: block[i // 2, 2 * (i % 2) + p // 4, p % 4],
+                range(8),
+                lambda xx: halves[lax.rem(y, 2), xx, pl.ds(y // 2, 1), :],
+            )
             write_lines(msg, it, lines)
-            tell(it)
+            for i in range(2):
+                msg_half[n, i : i + 1] = msg[it, 2 * i : 2 * i + 1] + msg[it, 2 * i + 1 : 2 * i + 2]
+            for peer in plane:
+                remote(msg_half.at[n], inbox_half.at[n, 2 * y + c, x], m_send.at[it], m_recv.at[it], peer).start()
+            inbox_half[n, 2 * y + c, x] = msg_half[n]
             if it == ITERS - 1:
 
                 @pl.when(giver)
@@ -457,15 +505,17 @@
                     w, t = out_tile(0)
                     out_block[...] = block[w, t]
 
-
                 @pl.when(jnp.logical_not(giver))
                 def _():
                     give(1).wait_recv()
 
                 start(store_schur)
-            state = update(it, state, heard(it))
-    for i in range(SIDE):
-        final[i // 2, 4 * (i % 2) : 4 * (i % 2) + 4] = state[0][i]
+            state = update(it, state, heard_halves(n, it))
+    for xx in range(SIDE):
+        for i in range(2):
+            for p in range(2):
+                row = 4 * (xx % 2) + 2 * i + p
+                final[xx // 2, row : row + 1, :] = state[0][p, xx, i : i + 1, :]
     store_answer.start()
 
     with jax.named_scope("finish"):
@@ -477,7 +527,7 @@
         landed(far_in, fb_send)
         landed(near_in, nb_send)
         for it in range(ITERS):
-            landed(tally, m_send.at[it])
+            landed(tally if it < EARLY else tally_half, m_send.at[it])
         for it in range(EARLY):
             landed(deep_tally, z_send.at[it])
 
@@ -522,10 +572,14 @@
             pltpu.VMEM((2, 8, T), F32),
             pltpu.VMEM((SIDE, SIDE, T), F32),
             pltpu.VMEM((ITERS, SIDE, T), F32),
-            pltpu.VMEM((ITERS, 8, SIDE, SIDE, T), F32),
+            pltpu.VMEM((EARLY, 8, SIDE, SIDE, T), F32),
             pltpu.VMEM((EARLY, SIDE, T), F32),
             pltpu.VMEM((EARLY, DEPTH, SIDE, T), F32),
             pltpu.VMEM((31, SIDE, T), F32),
+            pltpu.VMEM((2, SIDE, 2, T), F32),
+            pltpu.VMEM((ITERS - EARLY, 2, T), F32),
+            pltpu.VMEM((ITERS - EARLY, 8, SIDE, 2, T), F32),
+            pltpu.VMEM((31, 2, T), F32),
             dma((KS + 7,)),
             dma((2,)),
             dma((2, KS)),
@@ -545,7 +599,7 @@
             dma((ITERS,)),
             dma((EARLY,)),
             dma((EARLY,)),
-            pltpu.SemaphoreType.REGULAR((2,)),
+            pltpu.SemaphoreType.REGULAR((7,)),
         ],
         compiler_params=pltpu.CompilerParams(
             collective_id=0, has_side_effects=True, vmem_limit_bytes=67_043_328

time: 91.4 us -> 91 us (level)
  no operation moved by 1% of the time
where the time goes in v6:
time: 91 us; the launch traced here: 90.8 us
  Pallas kernels  87.5 us (96%)
  local copies, waits for them, and re-layouts  2.67 us (3%)
    pallas_call x1, Pallas kernels, on_device(): pl.pallas_call(kernel, out_shape=jax.ShapeDtypeStruct((10, 8, T), F32), i...  87.5 us
    reshape x2, local copies, waits for them, and re-layouts, on_device(): return (out[:8].reshape(8 * SUB, T), out[8:].reshape(SIDE * SIDE * T))  2.67 us

profile of v6, /device:TPU:1, one launch (start us, length us, event | category | flops | bytes accessed | tf_op | source)
XLA Modules:
  0.0 90.8 jit_solution(15649688035529486828)
XLA Ops:
  0.6 87.5 %shard_map.86 = f32[10,8,128]{2,1,0:T(8,128)} custom-call(s32[1,6]{1,0:T(1,128)} %bitcast.13, f32[1,192]{1,0:T(1,128)} %bitcast.12, s32[16,192]{1,0:T(8,128)} %bitcast.9, bf16[6,512,128]{2,1,0:T(8,128)(2,1)} %b_hbm.1, f32[6,512]{1,0:T(8,128)} %rs_hbm.1, f32[4,4,128]{2,1,0:T(4,128)} %bitcast.10, f32[4,4,128]{2,1,0:T(4,128)} %bitcast.11), custom_call_target="tpu_custom_call" | custom-call | tf_op jit(solution)/shard_map/pallas_call | solution.py:545
  88.1 1.3 %slice_bitcast_fusion.1 = f32[2048]{0:T(1024)} fusion(f32[10,8,128]{2,1,0:T(8,128)} %shard_map.86), kind=kLoop, calls=%fused_computation.1 | loop fusion | bytes 16384 | tf_op jit(solution)/shard_map/reshape | solution.py:616
  89.4 1.4 %slice_bitcast_fusion = f32[64,128]{1,0:T(8,128)} fusion(f32[10,8,128]{2,1,0:T(8,128)} %shard_map.86), kind=kLoop, calls=%fused_computation | loop fusion | bytes 65536 | tf_op jit(solution)/shard_map/reshape | solution.py:616

commit v7 on v6

--- a/solution.py
+++ b/solution.py
@@ -36,7 +36,8 @@
     rs_hbm,
     fd_hbm,
     rhs_hbm,
-    out_hbm,
+    schur_hbm,
+    answer_hbm,
     assign_ref,
     prob_ref,
     pattern_ref,
@@ -446,10 +447,8 @@
     rel = lax.rem(m + SIDE - y, SIDE)
     out_row = jnp.where(rel == 2, 3, jnp.where(rel == 3, 2, rel))
     giver = x == q
-    store_schur = tuple(
-        pltpu.make_async_copy(out_block.at[i], out_hbm.at[pl.ds(4 * i, 4)], in_sem.at[i]) for i in range(2)
-    )
-    store_answer = pltpu.make_async_copy(final, out_hbm.at[pl.ds(8, 2)], in_sem.at[2])
+    store_schur = (pltpu.make_async_copy(out_block, schur_hbm, in_sem.at[0]),)
+    store_answer = pltpu.make_async_copy(final, answer_hbm, in_sem.at[2])
 
     def out_tile(pc):
         idx = INDEX[0, pc]
@@ -542,11 +541,14 @@
 def on_device(borders, row_scale, assign, prob, pattern, first_diag, rhs):
     held = pl.BlockSpec(memory_space=pltpu.HBM)
     dma = pltpu.SemaphoreType.DMA
-    out = pl.pallas_call(
+    schur, answer = pl.pallas_call(
         kernel,
-        out_shape=jax.ShapeDtypeStruct((10, 8, T), F32),
+        out_shape=(
+            jax.ShapeDtypeStruct((2, 4, SUB, T), F32),
+            jax.ShapeDtypeStruct((2, 8, T), F32),
+        ),
         in_specs=[held] * 7,
-        out_specs=held,
+        out_specs=(held, held),
         scratch_shapes=[
             pltpu.VMEM((1, KS), jnp.int32),
             pltpu.VMEM((1, SCEN), F32),
@@ -613,7 +615,7 @@
         first_diag.reshape(SIDE, SIDE, T),
         rhs.reshape(SIDE, SIDE, T),
     )
-    return out[:8].reshape(8 * SUB, T), out[8:].reshape(SIDE * SIDE * T)
+    return schur.reshape(8 * SUB, T), answer.reshape(SIDE * SIDE * T)
 
 
 def solution(mesh):

time: 91 us -> 90.3 us (level)
    reshape x2 -> x0, local copies, waits for them, and re-layouts: 2.67 us -> none  [on_device(): return (out[:8].reshape(8 * SUB, T), out[8:].reshape(SIDE * SIDE * T))]
    unnamed x0 -> x4, local copies, waits for them, and re-layouts: none -> 1.98 us
where the time goes in v7:
time: 90.3 us; the launch traced here: 90.1 us
  Pallas kernels  87.5 us (97%)
  local copies, waits for them, and re-layouts  1.98 us (2%)
    pallas_call x1, Pallas kernels, on_device(): pl.pallas_call(kernel, out_shape=(jax.ShapeDtypeStruct((2, 4, SUB, T), F3...  87.5 us
    unnamed x4, local copies, waits for them, and re-layouts  1.98 us

profile of v7, /device:TPU:1, one launch (start us, length us, event | category | flops | bytes accessed | tf_op | source)
XLA Modules:
  0.0 90.1 jit_solution(1552016170887425966)
XLA Ops:
  0.6 87.5 %shard_map.86 = (f32[2,4,8,128]{3,2,1,0:T(8,128)}, f32[2,8,128]{2,1,0:T(8,128)}) custom-call(s32[1,6]{1,0:T(1,128)} %bitcast.13, f32[1,192]{1,0:T(1,128)} %bitcast.12, s32[16,192]{1,0:T(8,128)} %bitcast.8, bf16[6,512,128]{2,1,0:T(8,128)(2,1)} %b_hbm.1, f32[6,512]{1,0:T(8,128)} %rs_hbm.1, f32[4,4,128]{2,1,0:T(4,128)} %bitcast.9, f32[4,4,128]{2,1,0:T(4,128)} %bitcast.10), custom_call_target="tpu_custom_call" | custom-call | tf_op jit(solution)/shard_map/pallas_call | solution.py:544
  88.1 0.0 copy-start
  88.1 1.4 %copy.11 = f32[64,128]{1,0:T(8,128)} copy(f32[64,128]{1,0:T(8,128)} %bitcast.7) | data formatting | bytes 65536
  89.5 0.0 copy-done
  89.5 0.6 copy.12
Async XLA Ops:
  88.1 1.4 %copy-start = (f32[2,8,128]{2,1,0:T(8,128)S(1)}, f32[2,8,128]{2,1,0:T(8,128)}, u32[]{:S(2)}) copy-start(f32[2,8,128]{2,1,0:T(8,128)} %get-tuple-element.5) | copy-start | bytes 24580
